TPU v7x, 128 devices: a whole 4x4x4 slice. The times are simulated.
128 devices in a mesh: gx: 4 (over x), gy: 8 (over z, y_lo), gz: 4 (over y_hi, core).
Axes of the slice: x: 4, y: 4 (y_hi: 2, y_lo: 2; y = y_hi * 2 + y_lo), z: 4, core: 2. Of those that a mesh axis runs over, the one named last changes fastest.
Arguments:
- tokens: bfloat16 [4096, 6144], P('gy', ('gz', 'gx')), may hold values from -6 to 6
- weight: bfloat16 [6144, 24576], P('gz', ('gx', 'gy')), may hold values from -0.15625 to 0.15625
- bias: float32 [24576], P(('gx', 'gz')), may hold values from -4 to 4
Outputs:
- hidden: bfloat16 [4096, 24576], P('gy', ('gx', 'gz'))
All inputs are finite; a program needn't handle non-finite values.
Results may differ from a plain program's by a relative error of at most 0.001.
Values may be sent and summed in bfloat16 or wider, within the bound.
No kernel may reach another device: no remote copies, remote signals or barrier semaphores. Data moves between devices by JAX's collectives and lax.ppermute only.
A program may use at most 128 MiB of HBM per device.

v0:
```python
import jax
import jax.numpy as jnp
from jax import lax
from jax.experimental import pallas as pl
from jax.experimental.pallas import tpu as pltpu
from jax.sharding import Mesh
from jax.sharding import PartitionSpec as P


NEAR = ((0, 256), (256, 128))
FAR = ((0, 0, 256), (1, 0, 128))
FORWARD = {"zn0": "both", "zn1": "both", "zf0": "both", "zf1": "both", "xo": "up", "xr1": "down", "xr2": "up"}
VMEM = pl.BlockSpec(memory_space=pltpu.VMEM)
ANY = pl.BlockSpec(memory_space=pl.ANY)
SWAP = [(0, 1), (1, 0)]


def shift(v, axis, step):
    return lax.ppermute(v, axis, [(i, (i + step) % 4) for i in range(4)])


def across(v, mask):
    if mask == 2:
        return lax.ppermute(v, "a", SWAP)
    if mask == 1:
        return lax.ppermute(v, "b", SWAP)
    return lax.ppermute(v, ("a", "b"), [(i, i ^ 3) for i in range(4)])


def places():
    return tuple(lax.axis_index(n) for n in ("x", "z", "a", "b", "c"))


def call(body, outs, vmem_args, extra=(), limit=4, scratch=(), out_spec=VMEM):
    args = [pltpu.with_memory_space_constraint(v, pltpu.VMEM) for v in vmem_args]
    return pl.pallas_call(
        body,
        out_shape=outs,
        in_specs=[VMEM] * len(args) + [ANY] * len(extra),
        out_specs=jax.tree.map(lambda _: out_spec, outs),
        scratch_shapes=scratch,
        compiler_params=pltpu.CompilerParams(vmem_limit_bytes=limit << 20),
    )(*args, *extra)


def vmem(shape, dtype):
    return pltpu.VMEM(shape, dtype)


def ring_gather(block, axis, tag):
    rows = block.shape[0] // 2
    lower = shift(block, axis, 1)
    upper = shift(block, axis, 3)
    mode = FORWARD[tag]
    if mode == "up":
        return block, lower, upper, shift(lower, axis, 1)
    if mode == "down":
        return block, lower, upper, shift(upper, axis, 3)

    def halves(low, upp, top, bottom):
        top[...] = low[0:rows, :]
        bottom[...] = upp[rows:, :]

    half = vmem((rows, block.shape[1]), block.dtype)
    top, bottom = call(halves, (half, half), [lower, upper])
    return block, lower, upper, shift(top, axis, 1), shift(bottom, axis, 3)


def prepare(weight, wanted):
    def body(w, *refs):
        outs, sems = refs[:-1], refs[-1]
        _, _, _, b, _ = places()
        copies = []
        for i, (own, start, width) in enumerate(wanted):
            at = pl.multiple_of((b if own else 1 - b) * 384 + start, 128)
            copies.append(pltpu.make_async_copy(w.at[:, pl.ds(at, width)], outs[i], sems.at[i]))
        for copy in copies:
            copy.start()
        for copy in copies:
            copy.wait()

    outs = tuple(vmem((1536, width), jnp.bfloat16) for _, _, width in wanted)
    weight = pltpu.with_memory_space_constraint(weight, pltpu.HBM)
    return call(body, outs, [], [weight], scratch=[pltpu.SemaphoreType.DMA((len(wanted),))])


def stack_rows(parts):
    def body(*refs):
        for i, ref in enumerate(refs[:-1]):
            refs[-1][i * 512 : (i + 1) * 512, :] = ref[...]

    return call(body, vmem((512 * len(parts), 384), jnp.bfloat16), parts)


def assemble(pieces, count):
    def body(*refs):
        ins, outs = refs[: len(pieces)], refs[len(pieces) :]
        x = places()[0]
        for step, group in ((0, ins[:1]), (3, ins[1:2]), (1, ins[2:3]), (2, ins[3:])):
            at = pl.multiple_of(((x + step) % 4) * 384, 128)
            row = 0
            for ref in group:
                for i, out in enumerate(outs):
                    first, last = max(row, i * 512), min(row + ref.shape[0], (i + 1) * 512)
                    if first < last:
                        out[first - i * 512 : last - i * 512, pl.ds(at, 384)] = ref[first - row : last - row, :]
                row += ref.shape[0]

    return call(body, (vmem((512, 1536), jnp.bfloat16),) * count, list(pieces))


def sides(w0, w1, w2, *w3):
    return (
        lambda: jnp.concatenate([w0[...], jnp.concatenate([w[...] for w in w3], 0) if len(w3) > 1 else w3[0][...]], 1),
        lambda: jnp.concatenate([w1[...], w2[...]], 1),
    )


def near_sums(rows, blocks, width):
    def body(a, *refs):
        blocks, out = refs[:-1], refs[-1]
        for i, side in enumerate(sides(*blocks)):
            out[i] = jnp.dot(a[...], side(), preferred_element_type=jnp.float32)

    return call(body, vmem((2, 512, 2 * width), jnp.float32), [rows, *blocks])


def far_sums(sums, rows, blocks, chunk):
    near, offset, width = chunk
    apart = NEAR[near][1]

    def body(s, a, *refs):
        blocks, keep, send = refs[:-2], refs[-2], refs[-1]
        _, z, _, b, c = places()
        even, odd = sides(*blocks)

        def fill(parity, side, owner, target):
            first = ((owner % 4) // 2 + b) % 2
            total = jnp.dot(a[...], side(), preferred_element_type=jnp.float32)
            target[first] = total[:, :width] + s[parity, :, offset : offset + width]
            target[1 - first] = total[:, width:] + s[parity, :, apart + offset : apart + offset + width]

        @pl.when(z % 2 == c)
        def _():
            fill(1, odd, z + 3, send)
            fill(0, even, z, keep)

        @pl.when(z % 2 != c)
        def _():
            fill(0, even, z, send)
            fill(1, odd, z + 3, keep)

    shape = vmem((2, 512, width), jnp.float32)
    return call(body, (shape, shape), [sums, rows, *blocks])


def activate(keep, other, mine, theirs, chunk):
    near, offset, width = chunk

    def body(k, o, bias_near, bias_far, *outs):
        _, _, a, b, _ = places()
        row = a * 6 + b * 3 + (NEAR[near][0] + offset) // 128
        for rb, bias_ref in enumerate((bias_near, bias_far)):
            for j in range(width // 128):
                cols = slice(j * 128, (j + 1) * 128)
                shift_by = bias_ref[pl.ds(row + j, 1), :]

                def step(i, carry):
                    at = pl.multiple_of(i * 64, 64)
                    v = k[rb, pl.ds(at, 64), cols] + o[rb, pl.ds(at, 64), cols] + shift_by
                    hidden = 0.5 * v * (1.0 + lax.erf(v * 0.7071067811865476))
                    outs[rb][pl.ds(at, 64), cols] = hidden.astype(jnp.bfloat16)
                    return carry

                lax.fori_loop(0, 8, step, 0)

    return call(body, (vmem((512, width), jnp.bfloat16),) * 2, [keep, other, mine, theirs])


def lay_out(pieces):
    def body(*refs):
        blocks, out, sems = refs[:-2], refs[-2], refs[-1]
        _, _, a, b, _ = places()
        copies = []
        for k, (near, offset, width) in enumerate(FAR):
            for mask in range(4):
                fa, phi = (a + mask // 2) % 2, (b + mask % 2) % 2
                at = pl.multiple_of(fa * 768 + phi * 384 + NEAR[near][0] + offset, 128)
                i = k * 4 + mask
                copies.append(pltpu.make_async_copy(blocks[i], out.at[:, pl.ds(at, width)], sems.at[i]))
        for copy in copies:
            copy.start()
        for copy in copies:
            copy.wait()

    out = jax.ShapeDtypeStruct((512, 1536), jnp.bfloat16)
    return call(body, out, pieces, scratch=[pltpu.SemaphoreType.DMA((len(pieces),))], out_spec=ANY)


def per_device_in_order(tokens, weight, bias):
    bias = bias.reshape(12, 128)
    own0 = prepare(weight, [(True, *NEAR[0])])
    spans = [(NEAR[near][0] + offset, width) for near, offset, width in FAR]
    own1, *give = prepare(weight, [(True, *NEAR[1])] + [(False, *span) for span in spans])

    near = [ring_gather(block, "z", f"zn{h}") for h, block in enumerate((*own0, own1))]
    ta, tb, tab = (across(tokens, mask) for mask in (2, 1, 3))
    tok_own = ring_gather(tokens, "x", "xo")
    got = [across(block, 1) for block in give]
    theirs = across(bias, 1)
    tok_one = ring_gather(stack_rows([ta, tab]), "x", "xr1")
    tok_two = ring_gather(tb, "x", "xr2")
    far = [ring_gather(block, "z", f"zf{k}") for k, block in enumerate(got)]

    (near_own,) = assemble(tok_own, 1)
    near_across, far_across = assemble(tok_one, 2)
    (far_own,) = assemble(tok_two, 1)
    sums = {}
    for h, (_, width) in enumerate(NEAR):
        for ra, rows in ((0, near_own), (1, near_across)):
            sums[h, ra] = near_sums(rows, near[h], width)

    pieces = []
    for k, chunk in enumerate(FAR):
        blocks = {}
        for ra, rows in ((1, far_across), (0, far_own)):
            keep, send = far_sums(sums[chunk[0], ra], rows, far[k], chunk)
            other = lax.ppermute(send, "c", SWAP)
            blocks[ra] = activate(keep, other, bias, theirs, chunk)
        pieces += [blocks[0][0], across(blocks[0][1], 1), across(blocks[1][0], 2), across(blocks[1][1], 3)]
    return lay_out(pieces)


def solution(mesh):
    torus = Mesh(mesh.devices.reshape(4, 4, 2, 2, 2), ("x", "z", "a", "b", "c"))
    tokens_at = P(("z", "a"), ("b", "c", "x"))
    weight_at = P(("b", "c"), ("x", "z", "a"))
    bias_at = P(("x", "b", "c"))
    return jax.shard_map(
        per_device_in_order,
        mesh=torus,
        in_specs=(tokens_at, weight_at, bias_at),
        out_specs=P(("z", "a"), ("x", "b", "c")),
        check_vma=False,
    )
```

profile of v0, /device:TPU:1, one launch (start us, length us, event | category | flops | bytes accessed | tf_op | source)
XLA Modules:
  0.0 176.9 jit_solution(18286973812896963553)
XLA Ops:
  10.9 3.0 %collective-permute-start.7 = (bf16[512,384]{1,0:T(8,128)(2,1)S(1)}, bf16[512,384]{1,0:T(8,128)(2,1)S(1)}, u32[]{:S(2)}, u32[]{:S(2)}) collective-permute-start(bf16[512,384]{1,0:T(8,128)(2,1)S(1)} %copy-done), channel_id=1, source_target_pairs={{0,2},{2,0},{1,3},{3,1},{4,6},{6,4},{5,7},{7,5},{8,10},{10,8},{9,1... | collective-permute-start | bytes 1179656 | tf_op jit(solution)/shard_map/ppermute | solution.py:26
  13.9 31.5 %collective-permute-done.20.refs_1_ = bf16[512,384]{1,0:T(8,128)(2,1)S(1)} collective-permute-done((bf16[512,384]{1,0:T(8,128)(2,1)}, bf16[512,384]{1,0:T(8,128)(2,1)S(1)}, u32[]{:S(2)}, u32[]{:S(2)}) %collective-permute-start.20) | collective-permute-done | bytes 393248 | tf_op jit(solution)/shard_map/ppermute | solution.py:27
  45.4 2.5 %collective-permute-start.1 = (bf16[512,384]{1,0:T(8,128)(2,1)S(1)}, bf16[512,384]{1,0:T(8,128)(2,1)S(1)}, u32[]{:S(2)}, u32[]{:S(2)}) collective-permute-start(bf16[512,384]{1,0:T(8,128)(2,1)S(1)} %copy-done), channel_id=1, source_target_pairs={{0,96},{32,0},{64,32},{96,64},{1,97},{33,1},{65,33},{97,65},{2,98}... | collective-permute-start | bytes 1179656 | tf_op jit(solution)/shard_map/ppermute | solution.py:19
  51.0 3.4 %collective-permute-done.1.refs_2_ = bf16[512,384]{1,0:T(8,128)(2,1)S(1)} collective-permute-done((bf16[512,384]{1,0:T(8,128)(2,1)S(1)}, bf16[512,384]{1,0:T(8,128)(2,1)S(1)}, u32[]{:S(2)}, u32[]{:S(2)}) %collective-permute-start.1) | collective-permute-done | bytes 393248 | tf_op jit(solution)/shard_map/ppermute | solution.py:19
  54.4 3.4 %collective-permute-start.22 = (bf16[1024,384]{1,0:T(8,128)(2,1)S(1)}, bf16[1024,384]{1,0:T(8,128)(2,1)S(1)}, u32[]{:S(2)}, u32[]{:S(2)}) collective-permute-start(bf16[1024,384]{1,0:T(8,128)(2,1)S(1)} %shard_map.46.refs_0_), channel_id=1, source_target_pairs={{0,96},{32,0},{64,32},{96,64},{1,97},{33,1},{65,33},{97,65},{2,98}... | collective-permute-start | bytes 2359304 | tf_op jit(solution)/shard_map/ppermute | solution.py:19
  57.8 3.8 %collective-permute-start.4 = (bf16[1536,256]{1,0:T(8,128)(2,1)S(1)}, bf16[1536,256]{1,0:T(8,128)(2,1)S(1)}, u32[]{:S(2)}, u32[]{:S(2)}) collective-permute-start(bf16[1536,256]{1,0:T(8,128)(2,1)S(1)} %shard_map.38.refs_0_), channel_id=1, source_target_pairs={{0,24},{8,0},{16,8},{24,16},{1,25},{9,1},{17,9},{25,17},{2,26},{10... | collective-permute-start | bytes 2359304 | tf_op jit(solution)/shard_map/ppermute | solution.py:19
  61.6 4.4 %collective-permute-done.8.refs_1_ = bf16[512,384]{1,0:T(8,128)(2,1)S(1)} collective-permute-done((bf16[512,384]{1,0:T(8,128)(2,1)S(1)}, bf16[512,384]{1,0:T(8,128)(2,1)S(1)}, u32[]{:S(2)}, u32[]{:S(2)}) %collective-permute-start.8) | collective-permute-done | bytes 393248 | tf_op jit(solution)/shard_map/ppermute | solution.py:19
  66.0 3.8 %collective-permute-start.13 = (bf16[1536,256]{1,0:T(8,128)(2,1)S(1)}, bf16[1536,256]{1,0:T(8,128)(2,1)S(1)}, u32[]{:S(2)}, u32[]{:S(2)}) collective-permute-start(bf16[1536,256]{1,0:T(8,128)(2,1)S(1)} %collective-permute-done.11.refs_0_), channel_id=1, source_target_pairs={{0,24},{8,0},{16,8},{24,16},{1,25},{9,1},{17,9},{25,17},{2,26},{10... | collective-permute-start | bytes 2359304 | tf_op jit(solution)/shard_map/ppermute | solution.py:19
  71.9 3.4 %collective-permute-start.23 = (bf16[1024,384]{1,0:T(8,128)(2,1)S(1)}, bf16[1024,384]{1,0:T(8,128)(2,1)S(1)}, u32[]{:S(2)}, u32[]{:S(2)}) collective-permute-start(bf16[1024,384]{1,0:T(8,128)(2,1)S(1)} %collective-permute-done.22.refs_2_), channel_id=1, source_target_pairs={{0,96},{32,0},{64,32},{96,64},{1,97},{33,1},{65,33},{97,65},{2,98}... | collective-permute-start | bytes 2359304 | tf_op jit(solution)/shard_map/ppermute | solution.py:19
  75.4 10.0 %collective-permute-done.12.low.refs_1_ = bf16[1536,256]{1,0:T(8,128)(2,1)S(1)} collective-permute-done((bf16[1536,256]{1,0:T(8,128)(2,1)S(1)}, bf16[1536,256]{1,0:T(8,128)(2,1)S(1)}, u32[]{:S(2)}, u32[]{:S(2)}) %collective-permute-start.12) | collective-permute-done | bytes 786464 | tf_op jit(solution)/shard_map/ppermute | solution.py:19
  85.4 4.4 %collective-permute-done.13.upp.refs_2_ = bf16[1536,256]{1,0:T(8,128)(2,1)S(1)} collective-permute-done((bf16[1536,256]{1,0:T(8,128)(2,1)S(1)}, bf16[1536,256]{1,0:T(8,128)(2,1)S(1)}, u32[]{:S(2)}, u32[]{:S(2)}) %collective-permute-start.13) | collective-permute-done | bytes 786464 | tf_op jit(solution)/shard_map/ppermute | solution.py:19
  89.8 3.4 %collective-permute-start.6 = (bf16[768,256]{1,0:T(8,128)(2,1)S(1)}, bf16[768,256]{1,0:T(8,128)(2,1)S(1)}, u32[]{:S(2)}, u32[]{:S(2)}) collective-permute-start(bf16[768,256]{1,0:T(8,128)(2,1)S(1)} %get-tuple-element.35), channel_id=1, source_target_pairs={{0,24},{8,0},{16,8},{24,16},{1,25},{9,1},{17,9},{25,17},{2,26},{10... | collective-permute-start | bytes 1179656 | tf_op jit(solution)/shard_map/ppermute | solution.py:19
  93.3 3.7 %collective-permute-done.9.refs_2_ = bf16[512,384]{1,0:T(8,128)(2,1)S(1)} collective-permute-done((bf16[512,384]{1,0:T(8,128)(2,1)S(1)}, bf16[512,384]{1,0:T(8,128)(2,1)S(1)}, u32[]{:S(2)}, u32[]{:S(2)}) %collective-permute-start.9) | collective-permute-done | bytes 393248 | tf_op jit(solution)/shard_map/ppermute | solution.py:19
  100.9 2.7 %collective-permute-start.28 = (bf16[1536,128]{1,0:T(8,128)(2,1)S(1)}, bf16[1536,128]{1,0:T(8,128)(2,1)S(1)}, u32[]{:S(2)}, u32[]{:S(2)}) collective-permute-start(bf16[1536,128]{1,0:T(8,128)(2,1)S(1)} %get-tuple-element.49.refs_0_), channel_id=1, source_target_pairs={{0,24},{8,0},{16,8},{24,16},{1,25},{9,1},{17,9},{25,17},{2,26},{10... | collective-permute-start | bytes 1179656 | tf_op jit(solution)/shard_map/ppermute | solution.py:19
  103.5 2.4 %collective-permute-done.14.refs_3_ = bf16[768,256]{1,0:T(8,128)(2,1)S(1)} collective-permute-done((bf16[768,256]{1,0:T(8,128)(2,1)S(1)}, bf16[768,256]{1,0:T(8,128)(2,1)S(1)}, u32[]{:S(2)}, u32[]{:S(2)}) %collective-permute-start.14) | collective-permute-done | bytes 393248 | tf_op jit(solution)/shard_map/ppermute | solution.py:19
  105.9 4.0 %collective-permute-done.15.refs_4_ = bf16[768,256]{1,0:T(8,128)(2,1)S(1)} collective-permute-done((bf16[768,256]{1,0:T(8,128)(2,1)S(1)}, bf16[768,256]{1,0:T(8,128)(2,1)S(1)}, u32[]{:S(2)}, u32[]{:S(2)}) %collective-permute-start.15) | collective-permute-done | bytes 393248 | tf_op jit(solution)/shard_map/ppermute | solution.py:19
  115.9 11.9 %collective-permute-start.24 = (f32[2,512,256]{2,1,0:T(8,128)S(1)}, f32[2,512,256]{2,1,0:T(8,128)S(1)}, u32[]{:S(2)}, u32[]{:S(2)}) collective-permute-start(f32[2,512,256]{2,1,0:T(8,128)S(1)} %get-tuple-element.46), channel_id=1, source_target_pairs={{0,1},{1,0},{2,3},{3,2},{4,5},{5,4},{6,7},{7,6},{8,9},{9,8},{10,11... | collective-permute-start | bytes 3145736 | tf_op jit(solution)/shard_map/ppermute | solution.py:228
  131.9 2.7 %collective-permute-start.30 = (bf16[768,128]{1,0:T(8,128)(2,1)S(1)}, bf16[768,128]{1,0:T(8,128)(2,1)S(1)}, u32[]{:S(2)}, u32[]{:S(2)}) collective-permute-start(bf16[768,128]{1,0:T(8,128)(2,1)S(1)} %get-tuple-element.51), channel_id=1, source_target_pairs={{0,24},{8,0},{16,8},{24,16},{1,25},{9,1},{17,9},{25,17},{2,26},{10... | collective-permute-start | bytes 589832 | tf_op jit(solution)/shard_map/ppermute | solution.py:19
  134.7 4.4 %collective-permute-done.29.refs_3_ = bf16[768,128]{1,0:T(8,128)(2,1)S(1)} collective-permute-done((bf16[768,128]{1,0:T(8,128)(2,1)S(1)}, bf16[768,128]{1,0:T(8,128)(2,1)S(1)}, u32[]{:S(2)}, u32[]{:S(2)}) %collective-permute-start.29) | collective-permute-done | bytes 196640 | tf_op jit(solution)/shard_map/ppermute | solution.py:19
  140.1 3.2 %collective-permute-done.34.refs_3_ = bf16[768,128]{1,0:T(8,128)(2,1)S(1)} collective-permute-done((bf16[768,128]{1,0:T(8,128)(2,1)S(1)}, bf16[768,128]{1,0:T(8,128)(2,1)S(1)}, u32[]{:S(2)}, u32[]{:S(2)}) %collective-permute-start.34) | collective-permute-done | bytes 196640 | tf_op jit(solution)/shard_map/ppermute | solution.py:19
  144.9 3.2 %collective-permute-start.36 = (f32[2,512,128]{2,1,0:T(8,128)S(1)}, f32[2,512,128]{2,1,0:T(8,128)S(1)}, u32[]{:S(2)}, u32[]{:S(2)}) collective-permute-start(f32[2,512,128]{2,1,0:T(8,128)S(1)} %get-tuple-element.56), channel_id=1, source_target_pairs={{0,1},{1,0},{2,3},{3,2},{4,5},{5,4},{6,7},{7,6},{8,9},{9,8},{10,11... | collective-permute-start | bytes 1572872 | tf_op jit(solution)/shard_map/ppermute | solution.py:228
  150.3 4.0 %collective-permute-done.17.bias_far = f32[12,128]{1,0:T(8,128)S(1)} collective-permute-done((f32[12,128]{1,0:T(8,128)S(1)}, f32[12,128]{1,0:T(8,128)S(1)}, u32[]{:S(2)}, u32[]{:S(2)}) %collective-permute-start.17) | collective-permute-done | bytes 6176 | tf_op jit(solution)/shard_map/ppermute | solution.py:26
  155.3 3.9 %collective-permute-start.25 = (bf16[512,256]{1,0:T(8,128)(2,1)S(1)}, bf16[512,256]{1,0:T(8,128)(2,1)S(1)}, u32[]{:S(2)}, u32[]{:S(2)}) collective-permute-start(bf16[512,256]{1,0:T(8,128)(2,1)S(1)} %get-tuple-element.47), channel_id=1, source_target_pairs={{0,4},{4,0},{1,5},{5,1},{2,6},{6,2},{3,7},{7,3},{8,12},{12,8},{9,1... | collective-permute-start | bytes 786440 | tf_op jit(solution)/shard_map/ppermute | solution.py:24
  163.5 11.1 %collective-permute-done.39.refs_6_ = bf16[512,128]{1,0:T(8,128)(2,1)S(1)} collective-permute-done((bf16[512,128]{1,0:T(8,128)(2,1)S(1)}, bf16[512,128]{1,0:T(8,128)(2,1)S(1)}, u32[]{:S(2)}, u32[]{:S(2)}) %collective-permute-start.39) | collective-permute-done | bytes 131104 | tf_op jit(solution)/shard_map/ppermute | solution.py:24
  (85 shorter events, 42.4 us)
Async XLA Ops:
  2.1 43.3 %collective-permute-start.20 = (bf16[512,384]{1,0:T(8,128)(2,1)}, bf16[512,384]{1,0:T(8,128)(2,1)S(1)}, u32[]{:S(2)}, u32[]{:S(2)}) collective-permute-start(bf16[512,384]{1,0:T(8,128)(2,1)} %refs_0_.1), channel_id=1, source_target_pairs={{0,6},{2,4},{4,2},{6,0},{1,7},{3,5},{5,3},{7,1},{8,14},{10,12},{12... | collective-permute-start | bytes 1179656 | tf_op jit(solution)/shard_map/ppermute | solution.py:27
  4.0 43.9 %collective-permute-start = (bf16[512,384]{1,0:T(8,128)(2,1)}, bf16[512,384]{1,0:T(8,128)(2,1)S(1)}, u32[]{:S(2)}, u32[]{:S(2)}) collective-permute-start(bf16[512,384]{1,0:T(8,128)(2,1)} %refs_0_.1), channel_id=1, source_target_pairs={{0,32},{32,64},{64,96},{96,0},{1,33},{33,65},{65,97},{97,1},{2,34}... | collective-permute-start | bytes 1179656 | tf_op jit(solution)/shard_map/ppermute | solution.py:19
  6.6 42.4 %collective-permute-start.31 = (bf16[1536,128]{1,0:T(8,128)(2,1)S(1)}, bf16[1536,128]{1,0:T(8,128)(2,1)S(1)}, u32[]{:S(2)}, u32[]{:S(2)}) collective-permute-start(bf16[1536,128]{1,0:T(8,128)(2,1)S(1)} %get-tuple-element.52), channel_id=1, source_target_pairs={{0,2},{2,0},{1,3},{3,1},{4,6},{6,4},{5,7},{7,5},{8,10},{10,8},{9,1... | collective-permute-start | bytes 1179656 | tf_op jit(solution)/shard_map/ppermute | solution.py:26
  7.4 54.2 %collective-permute-start.11 = (bf16[1536,256]{1,0:T(8,128)(2,1)S(1)}, bf16[1536,256]{1,0:T(8,128)(2,1)S(1)}, u32[]{:S(2)}, u32[]{:S(2)}) collective-permute-start(bf16[1536,256]{1,0:T(8,128)(2,1)S(1)} %get-tuple-element.36), channel_id=1, source_target_pairs={{0,2},{2,0},{1,3},{3,1},{4,6},{6,4},{5,7},{7,5},{8,10},{10,8},{9,1... | collective-permute-start | bytes 2359304 | tf_op jit(solution)/shard_map/ppermute | solution.py:26
  10.9 39.8 %collective-permute-start.7 = (bf16[512,384]{1,0:T(8,128)(2,1)S(1)}, bf16[512,384]{1,0:T(8,128)(2,1)S(1)}, u32[]{:S(2)}, u32[]{:S(2)}) collective-permute-start(bf16[512,384]{1,0:T(8,128)(2,1)S(1)} %copy-done), channel_id=1, source_target_pairs={{0,2},{2,0},{1,3},{3,1},{4,6},{6,4},{5,7},{7,5},{8,10},{10,8},{9,1... | collective-permute-start | bytes 1179656 | tf_op jit(solution)/shard_map/ppermute | solution.py:26
  49.1 20.7 %collective-permute-start.3 = (bf16[1536,256]{1,0:T(8,128)(2,1)S(1)}, bf16[1536,256]{1,0:T(8,128)(2,1)S(1)}, u32[]{:S(2)}, u32[]{:S(2)}) collective-permute-start(bf16[1536,256]{1,0:T(8,128)(2,1)S(1)} %shard_map.38.refs_0_), channel_id=1, source_target_pairs={{0,8},{8,16},{16,24},{24,0},{1,9},{9,17},{17,25},{25,1},{2,10},{10... | collective-permute-start | bytes 2359304 | tf_op jit(solution)/shard_map/ppermute | solution.py:19
  50.8 15.2 %collective-permute-start.8 = (bf16[512,384]{1,0:T(8,128)(2,1)S(1)}, bf16[512,384]{1,0:T(8,128)(2,1)S(1)}, u32[]{:S(2)}, u32[]{:S(2)}) collective-permute-start(bf16[512,384]{1,0:T(8,128)(2,1)S(1)} %collective-permute-done.7.refs_0_), channel_id=1, source_target_pairs={{0,32},{32,64},{64,96},{96,0},{1,33},{33,65},{65,97},{97,1},{2,34}... | collective-permute-start | bytes 1179656 | tf_op jit(solution)/shard_map/ppermute | solution.py:19
  54.4 17.5 %collective-permute-start.22 = (bf16[1024,384]{1,0:T(8,128)(2,1)S(1)}, bf16[1024,384]{1,0:T(8,128)(2,1)S(1)}, u32[]{:S(2)}, u32[]{:S(2)}) collective-permute-start(bf16[1024,384]{1,0:T(8,128)(2,1)S(1)} %shard_map.46.refs_0_), channel_id=1, source_target_pairs={{0,96},{32,0},{64,32},{96,64},{1,97},{33,1},{65,33},{97,65},{2,98}... | collective-permute-start | bytes 2359304 | tf_op jit(solution)/shard_map/ppermute | solution.py:19
  57.8 17.5 %collective-permute-start.4 = (bf16[1536,256]{1,0:T(8,128)(2,1)S(1)}, bf16[1536,256]{1,0:T(8,128)(2,1)S(1)}, u32[]{:S(2)}, u32[]{:S(2)}) collective-permute-start(bf16[1536,256]{1,0:T(8,128)(2,1)S(1)} %shard_map.38.refs_0_), channel_id=1, source_target_pairs={{0,24},{8,0},{16,8},{24,16},{1,25},{9,1},{17,9},{25,17},{2,26},{10... | collective-permute-start | bytes 2359304 | tf_op jit(solution)/shard_map/ppermute | solution.py:19
  61.6 23.8 %collective-permute-start.12 = (bf16[1536,256]{1,0:T(8,128)(2,1)S(1)}, bf16[1536,256]{1,0:T(8,128)(2,1)S(1)}, u32[]{:S(2)}, u32[]{:S(2)}) collective-permute-start(bf16[1536,256]{1,0:T(8,128)(2,1)S(1)} %collective-permute-done.11.refs_0_), channel_id=1, source_target_pairs={{0,8},{8,16},{16,24},{24,0},{1,9},{9,17},{17,25},{25,1},{2,10},{10... | collective-permute-start | bytes 2359304 | tf_op jit(solution)/shard_map/ppermute | solution.py:19
  66.0 23.9 %collective-permute-start.13 = (bf16[1536,256]{1,0:T(8,128)(2,1)S(1)}, bf16[1536,256]{1,0:T(8,128)(2,1)S(1)}, u32[]{:S(2)}, u32[]{:S(2)}) collective-permute-start(bf16[1536,256]{1,0:T(8,128)(2,1)S(1)} %collective-permute-done.11.refs_0_), channel_id=1, source_target_pairs={{0,24},{8,0},{16,8},{24,16},{1,25},{9,1},{17,9},{25,17},{2,26},{10... | collective-permute-start | bytes 2359304 | tf_op jit(solution)/shard_map/ppermute | solution.py:19
  69.7 28.9 %collective-permute-start.21 = (bf16[1024,384]{1,0:T(8,128)(2,1)S(1)}, bf16[1024,384]{1,0:T(8,128)(2,1)S(1)}, u32[]{:S(2)}, u32[]{:S(2)}) collective-permute-start(bf16[1024,384]{1,0:T(8,128)(2,1)S(1)} %shard_map.46.refs_0_), channel_id=1, source_target_pairs={{0,32},{32,64},{64,96},{96,0},{1,33},{33,65},{65,97},{97,1},{2,34}... | collective-permute-start | bytes 2359304 | tf_op jit(solution)/shard_map/ppermute | solution.py:19
  71.9 28.9 %collective-permute-start.23 = (bf16[1024,384]{1,0:T(8,128)(2,1)S(1)}, bf16[1024,384]{1,0:T(8,128)(2,1)S(1)}, u32[]{:S(2)}, u32[]{:S(2)}) collective-permute-start(bf16[1024,384]{1,0:T(8,128)(2,1)S(1)} %collective-permute-done.22.refs_2_), channel_id=1, source_target_pairs={{0,96},{32,0},{64,32},{96,64},{1,97},{33,1},{65,33},{97,65},{2,98}... | collective-permute-start | bytes 2359304 | tf_op jit(solution)/shard_map/ppermute | solution.py:19
  75.3 21.7 %collective-permute-start.9 = (bf16[512,384]{1,0:T(8,128)(2,1)S(1)}, bf16[512,384]{1,0:T(8,128)(2,1)S(1)}, u32[]{:S(2)}, u32[]{:S(2)}) collective-permute-start(bf16[512,384]{1,0:T(8,128)(2,1)S(1)} %collective-permute-done.7.refs_0_), channel_id=1, source_target_pairs={{0,96},{32,0},{64,32},{96,64},{1,97},{33,1},{65,33},{97,65},{2,98}... | collective-permute-start | bytes 1179656 | tf_op jit(solution)/shard_map/ppermute | solution.py:19
  85.4 15.3 %collective-permute-start.5 = (bf16[768,256]{1,0:T(8,128)(2,1)S(1)}, bf16[768,256]{1,0:T(8,128)(2,1)S(1)}, u32[]{:S(2)}, u32[]{:S(2)}) collective-permute-start(bf16[768,256]{1,0:T(8,128)(2,1)S(1)} %get-tuple-element.34), channel_id=1, source_target_pairs={{0,8},{8,16},{16,24},{24,0},{1,9},{9,17},{17,25},{25,1},{2,10},{10... | collective-permute-start | bytes 1179656 | tf_op jit(solution)/shard_map/ppermute | solution.py:19
  100.8 30.9 %collective-permute-start.27 = (bf16[1536,128]{1,0:T(8,128)(2,1)S(1)}, bf16[1536,128]{1,0:T(8,128)(2,1)S(1)}, u32[]{:S(2)}, u32[]{:S(2)}) collective-permute-start(bf16[1536,128]{1,0:T(8,128)(2,1)S(1)} %get-tuple-element.49.refs_0_), channel_id=1, source_target_pairs={{0,8},{8,16},{16,24},{24,0},{1,9},{9,17},{17,25},{25,1},{2,10},{10... | collective-permute-start | bytes 1179656 | tf_op jit(solution)/shard_map/ppermute | solution.py:19
  100.9 30.9 %collective-permute-start.28 = (bf16[1536,128]{1,0:T(8,128)(2,1)S(1)}, bf16[1536,128]{1,0:T(8,128)(2,1)S(1)}, u32[]{:S(2)}, u32[]{:S(2)}) collective-permute-start(bf16[1536,128]{1,0:T(8,128)(2,1)S(1)} %get-tuple-element.49.refs_0_), channel_id=1, source_target_pairs={{0,24},{8,0},{16,8},{24,16},{1,25},{9,1},{17,9},{25,17},{2,26},{10... | collective-permute-start | bytes 1179656 | tf_op jit(solution)/shard_map/ppermute | solution.py:19
  105.9 26.0 %collective-permute-start.32 = (bf16[1536,128]{1,0:T(8,128)(2,1)S(1)}, bf16[1536,128]{1,0:T(8,128)(2,1)S(1)}, u32[]{:S(2)}, u32[]{:S(2)}) collective-permute-start(bf16[1536,128]{1,0:T(8,128)(2,1)S(1)} %collective-permute-done.31.refs_0_), channel_id=1, source_target_pairs={{0,8},{8,16},{16,24},{24,0},{1,9},{9,17},{17,25},{25,1},{2,10},{10... | collective-permute-start | bytes 1179656 | tf_op jit(solution)/shard_map/ppermute | solution.py:19
  109.9 24.6 %collective-permute-start.33 = (bf16[1536,128]{1,0:T(8,128)(2,1)S(1)}, bf16[1536,128]{1,0:T(8,128)(2,1)S(1)}, u32[]{:S(2)}, u32[]{:S(2)}) collective-permute-start(bf16[1536,128]{1,0:T(8,128)(2,1)S(1)} %collective-permute-done.31.refs_0_), channel_id=1, source_target_pairs={{0,24},{8,0},{16,8},{24,16},{1,25},{9,1},{17,9},{25,17},{2,26},{10... | collective-permute-start | bytes 1179656 | tf_op jit(solution)/shard_map/ppermute | solution.py:19
  115.9 38.8 %collective-permute-start.24 = (f32[2,512,256]{2,1,0:T(8,128)S(1)}, f32[2,512,256]{2,1,0:T(8,128)S(1)}, u32[]{:S(2)}, u32[]{:S(2)}) collective-permute-start(f32[2,512,256]{2,1,0:T(8,128)S(1)} %get-tuple-element.46), channel_id=1, source_target_pairs={{0,1},{1,0},{2,3},{3,2},{4,5},{5,4},{6,7},{7,6},{8,9},{9,8},{10,11... | collective-permute-start | bytes 3145736 | tf_op jit(solution)/shard_map/ppermute | solution.py:228
  131.7 27.6 %collective-permute-start.16 = (f32[2,512,256]{2,1,0:T(8,128)S(1)}, f32[2,512,256]{2,1,0:T(8,128)S(1)}, u32[]{:S(2)}, u32[]{:S(2)}) collective-permute-start(f32[2,512,256]{2,1,0:T(8,128)S(1)} %get-tuple-element.40), channel_id=1, source_target_pairs={{0,1},{1,0},{2,3},{3,2},{4,5},{5,4},{6,7},{7,6},{8,9},{9,8},{10,11... | collective-permute-start | bytes 3145736 | tf_op jit(solution)/shard_map/ppermute | solution.py:228
  155.3 20.2 %collective-permute-start.25 = (bf16[512,256]{1,0:T(8,128)(2,1)S(1)}, bf16[512,256]{1,0:T(8,128)(2,1)S(1)}, u32[]{:S(2)}, u32[]{:S(2)}) collective-permute-start(bf16[512,256]{1,0:T(8,128)(2,1)S(1)} %get-tuple-element.47), channel_id=1, source_target_pairs={{0,4},{4,0},{1,5},{5,1},{2,6},{6,2},{3,7},{7,3},{8,12},{12,8},{9,1... | collective-permute-start | bytes 786440 | tf_op jit(solution)/shard_map/ppermute | solution.py:24
  159.2 16.3 %collective-permute-start.26 = (bf16[512,256]{1,0:T(8,128)(2,1)S(1)}, bf16[512,256]{1,0:T(8,128)(2,1)S(1)}, u32[]{:S(2)}, u32[]{:S(2)}) collective-permute-start(bf16[512,256]{1,0:T(8,128)(2,1)S(1)} %get-tuple-element.48), channel_id=1, source_target_pairs={{0,6},{2,4},{4,2},{6,0},{1,7},{3,5},{5,3},{7,1},{8,14},{10,12},{12... | collective-permute-start | bytes 786440 | tf_op jit(solution)/shard_map/ppermute | solution.py:27
  159.8 15.7 %collective-permute-start.18 = (bf16[512,256]{1,0:T(8,128)(2,1)S(1)}, bf16[512,256]{1,0:T(8,128)(2,1)S(1)}, u32[]{:S(2)}, u32[]{:S(2)}) collective-permute-start(bf16[512,256]{1,0:T(8,128)(2,1)S(1)} %get-tuple-element.42), channel_id=1, source_target_pairs={{0,2},{2,0},{1,3},{3,1},{4,6},{6,4},{5,7},{7,5},{8,10},{10,8},{9,1... | collective-permute-start | bytes 786440 | tf_op jit(solution)/shard_map/ppermute | solution.py:26
  (19 other events, 174.8 us)
where the time goes:
time: 178 us; the launch traced here: 177 us
  waiting for transfers between devices  91.4 us (51%)
  starting transfers between devices  67.4 us (38%)
  Pallas kernels  17.7 us (10%)
    ppermute x25, waiting for transfers between devices, shift(): return lax.ppermute(v, axis, [(i, (i + step) % 4) for i in range(4)])  42.7 us
    ppermute x25, starting transfers between devices, shift(): return lax.ppermute(v, axis, [(i, (i + step) % 4) for i in range(4)])  34.5 us
    ppermute x3, waiting for transfers between devices, across(): return lax.ppermute(v, ('a', 'b'), [(i, i ^ 3) for i in range(4)])  32.3 us
    pallas_call x23, Pallas kernels, call(): pl.pallas_call(body, out_shape=outs, in_specs=[VMEM] * len(args) + [ANY]...  17.7 us
    ppermute x4, starting transfers between devices, per_device_in_order(): other = lax.ppermute(send, 'c', SWAP)  15.3 us
    ppermute x3, waiting for transfers between devices, across(): return lax.ppermute(v, 'a', SWAP)  12.4 us
    ppermute x6, starting transfers between devices, across(): return lax.ppermute(v, 'b', SWAP)  8.18 us
    ppermute x3, starting transfers between devices, across(): return lax.ppermute(v, 'a', SWAP)  7.49 us
  transfers between devices with their start and end apart: 41, of which 16 were waited for; matrix products, arithmetic and copies ran while one was open for 0% of the time, Pallas kernels for 9%

commit v1 on v0

--- a/solution.py
+++ b/solution.py
@@ -9,7 +9,7 @@
 
 NEAR = ((0, 256), (256, 128))
 FAR = ((0, 0, 256), (1, 0, 128))
-FORWARD = {"zn0": "both", "zn1": "both", "zf0": "both", "zf1": "both", "xo": "up", "xr1": "down", "xr2": "up"}
+FORWARD = {"zn0": "core", "zn1": "core", "zf0": "both", "zf1": "both", "xo": "core", "xr1": "core", "xr2": "core"}
 VMEM = pl.BlockSpec(memory_space=pltpu.VMEM)
 ANY = pl.BlockSpec(memory_space=pl.ANY)
 SWAP = [(0, 1), (1, 0)]
@@ -31,7 +31,7 @@
     return tuple(lax.axis_index(n) for n in ("x", "z", "a", "b", "c"))
 
 
-def call(body, outs, vmem_args, extra=(), limit=4, scratch=(), out_spec=VMEM):
+def call(body, outs, vmem_args, extra=(), limit=4, scratch=(), out_spec=VMEM, aliases=None):
     args = [pltpu.with_memory_space_constraint(v, pltpu.VMEM) for v in vmem_args]
     return pl.pallas_call(
         body,
@@ -39,6 +39,7 @@
         in_specs=[VMEM] * len(args) + [ANY] * len(extra),
         out_specs=jax.tree.map(lambda _: out_spec, outs),
         scratch_shapes=scratch,
+        input_output_aliases=aliases or {},
         compiler_params=pltpu.CompilerParams(vmem_limit_bytes=limit << 20),
     )(*args, *extra)
 
@@ -52,6 +53,22 @@
     lower = shift(block, axis, 1)
     upper = shift(block, axis, 3)
     mode = FORWARD[tag]
+    if mode == "core":
+
+        def pick(low, upp, out):
+            c = places()[4]
+
+            @pl.when(c == 0)
+            def _():
+                out[...] = low[...]
+
+            @pl.when(c != 0)
+            def _():
+                out[...] = upp[...]
+
+        chosen = call(pick, vmem(block.shape, block.dtype), [lower, upper])
+        pairs = [(2 * i + c, 2 * ((i + (1, 3)[c]) % 4) + c) for i in range(4) for c in (0, 1)]
+        return block, lower, upper, lax.ppermute(chosen, (axis, "c"), pairs)
     if mode == "up":
         return block, lower, upper, shift(lower, axis, 1)
     if mode == "down":
@@ -177,24 +194,26 @@
     return call(body, (vmem((512, width), jnp.bfloat16),) * 2, [keep, other, mine, theirs])
 
 
-def lay_out(pieces):
+def lay_out(pieces, chunk, filled=None):
+    near, offset, width = chunk
+
     def body(*refs):
-        blocks, out, sems = refs[:-2], refs[-2], refs[-1]
+        blocks, out, sems = refs[:4], refs[-2], refs[-1]
         _, _, a, b, _ = places()
         copies = []
-        for k, (near, offset, width) in enumerate(FAR):
-            for mask in range(4):
-                fa, phi = (a + mask // 2) % 2, (b + mask % 2) % 2
-                at = pl.multiple_of(fa * 768 + phi * 384 + NEAR[near][0] + offset, 128)
-                i = k * 4 + mask
-                copies.append(pltpu.make_async_copy(blocks[i], out.at[:, pl.ds(at, width)], sems.at[i]))
+        for mask in range(4):
+            fa, phi = (a + mask // 2) % 2, (b + mask % 2) % 2
+            at = pl.multiple_of(fa * 768 + phi * 384 + NEAR[near][0] + offset, 128)
+            copies.append(pltpu.make_async_copy(blocks[mask], out.at[:, pl.ds(at, width)], sems.at[mask]))
         for copy in copies:
             copy.start()
         for copy in copies:
             copy.wait()
 
     out = jax.ShapeDtypeStruct((512, 1536), jnp.bfloat16)
-    return call(body, out, pieces, scratch=[pltpu.SemaphoreType.DMA((len(pieces),))], out_spec=ANY)
+    scratch = [pltpu.SemaphoreType.DMA((4,))]
+    extra, aliases = ([], {}) if filled is None else ([filled], {4: 0})
+    return call(body, out, pieces, extra, scratch=scratch, out_spec=ANY, aliases=aliases)
 
 
 def per_device_in_order(tokens, weight, bias):
@@ -220,15 +239,16 @@
         for ra, rows in ((0, near_own), (1, near_across)):
             sums[h, ra] = near_sums(rows, near[h], width)
 
-    pieces = []
+    hidden = None
     for k, chunk in enumerate(FAR):
         blocks = {}
         for ra, rows in ((1, far_across), (0, far_own)):
             keep, send = far_sums(sums[chunk[0], ra], rows, far[k], chunk)
             other = lax.ppermute(send, "c", SWAP)
             blocks[ra] = activate(keep, other, bias, theirs, chunk)
-        pieces += [blocks[0][0], across(blocks[0][1], 1), across(blocks[1][0], 2), across(blocks[1][1], 3)]
-    return lay_out(pieces)
+        pieces = [blocks[0][0], across(blocks[0][1], 1), across(blocks[1][0], 2), across(blocks[1][1], 3)]
+        hidden = lay_out(pieces, chunk, hidden)
+    return hidden
 
 
 def solution(mesh):

time: 178 us -> 154 us (0.87)
  starting transfers between devices: 67.4 us -> 51.6 us
  waiting for transfers between devices: 91.4 us -> 83.8 us
    ppermute x3, waiting for transfers between devices: 12.4 us -> 0.01 us  [across(): return lax.ppermute(v, 'a', SWAP)]
    ppermute x4, starting transfers between devices: 15.3 us -> 4.97 us  [per_device_in_order(): other = lax.ppermute(send, 'c', SWAP)]
    ppermute x25 -> x18, starting transfers between devices: 34.5 us -> 24.8 us  [shift(): return lax.ppermute(v, axis, [(i, (i + step) % 4) for i in range(4)])]
    ppermute x0 -> x5, starting transfers between devices: none -> 7.74 us  [ring_gather(): return (block, lower, upper, lax.ppermute(chosen, (axis, 'c'), pairs))]
    ppermute x25 -> x18, waiting for transfers between devices: 42.7 us -> 50 us  [shift(): return lax.ppermute(v, axis, [(i, (i + step) % 4) for i in range(4)])]
    ppermute x3, waiting for transfers between devices: 32.3 us -> 26.7 us  [across(): return lax.ppermute(v, ('a', 'b'), [(i, i ^ 3) for i in range(4)])]
    ppermute x6, starting transfers between devices: 8.18 us -> 4.1 us  [across(): return lax.ppermute(v, 'b', SWAP)]
    ppermute x3, starting transfers between devices: 1.91 us -> 5.42 us  [across(): return lax.ppermute(v, ('a', 'b'), [(i, i ^ 3) for i in range(4)])]
  transfers between devices with their start and end apart: 41 -> 39, of which waited for: 16 -> 14; matrix products, arithmetic and copies ran while one was open for 0% -> 0% of each run, Pallas kernels for 9% -> 11%
where the time goes in v1:
time: 154 us
  waiting for transfers between devices  83.8 us (54%)
  starting transfers between devices  51.6 us (34%)
  Pallas kernels  18.4 us (12%)
    ppermute x18, waiting for transfers between devices, shift(): return lax.ppermute(v, axis, [(i, (i + step) % 4) for i in range(4)])  50 us
    ppermute x3, waiting for transfers between devices, across(): return lax.ppermute(v, ('a', 'b'), [(i, i ^ 3) for i in range(4)])  26.7 us
    ppermute x18, starting transfers between devices, shift(): return lax.ppermute(v, axis, [(i, (i + step) % 4) for i in range(4)])  24.8 us
    pallas_call x27, Pallas kernels, call(): pl.pallas_call(body, out_shape=outs, in_specs=[VMEM] * len(args) + [ANY]...  18.4 us
    ppermute x5, starting transfers between devices, ring_gather(): return (block, lower, upper, lax.ppermute(chosen, (axis, 'c'), pairs))  7.74 us
    ppermute x6, waiting for transfers between devices, across(): return lax.ppermute(v, 'b', SWAP)  5.51 us
    ppermute x3, starting transfers between devices, across(): return lax.ppermute(v, ('a', 'b'), [(i, i ^ 3) for i in range(4)])  5.42 us
    ppermute x4, starting transfers between devices, per_device_in_order(): other = lax.ppermute(send, 'c', SWAP)  4.97 us
  transfers between devices with their start and end apart: 39, of which 14 were waited for; matrix products, arithmetic and copies ran while one was open for 0% of the time, Pallas kernels for 11%

profile of v1, /device:TPU:1, one launch (start us, length us, event | category | flops | bytes accessed | tf_op | source)
XLA Modules:
  0.0 154.3 jit_solution(2844328340622720669)
XLA Ops:
  0.0 2.1 %collective-permute-start.18 = (bf16[512,384]{1,0:T(8,128)(2,1)}, bf16[512,384]{1,0:T(8,128)(2,1)S(1)}, u32[]{:S(2)}, u32[]{:S(2)}) collective-permute-start(bf16[512,384]{1,0:T(8,128)(2,1)} %refs_0_.1), channel_id=1, source_target_pairs={{0,4},{4,0},{1,5},{5,1},{2,6},{6,2},{3,7},{7,3},{8,12},{12,8},{9,1... | collective-permute-start | bytes 1179656 | tf_op jit(solution)/shard_map/ppermute | solution.py:24
  9.1 2.2 %collective-permute-start.27 = (bf16[1536,256]{1,0:T(8,128)(2,1)S(1)}, bf16[1536,256]{1,0:T(8,128)(2,1)S(1)}, u32[]{:S(2)}, u32[]{:S(2)}) collective-permute-start(bf16[1536,256]{1,0:T(8,128)(2,1)S(1)} %shard_map.53.refs_0_), channel_id=1, source_target_pairs={{0,24},{8,0},{16,8},{24,16},{1,25},{9,1},{17,9},{25,17},{2,26},{10... | collective-permute-start | bytes 2359304 | tf_op jit(solution)/shard_map/ppermute | solution.py:19
  11.3 17.3 %collective-permute-done.19.refs_1_ = bf16[512,384]{1,0:T(8,128)(2,1)S(1)} collective-permute-done((bf16[512,384]{1,0:T(8,128)(2,1)}, bf16[512,384]{1,0:T(8,128)(2,1)S(1)}, u32[]{:S(2)}, u32[]{:S(2)}) %collective-permute-start.19) | collective-permute-done | bytes 393248 | tf_op jit(solution)/shard_map/ppermute | solution.py:27
  33.0 2.2 %collective-permute-start.31 = (bf16[1536,256]{1,0:T(8,128)(2,1)S(1)}, bf16[1536,256]{1,0:T(8,128)(2,1)S(1)}, u32[]{:S(2)}, u32[]{:S(2)}) collective-permute-start(bf16[1536,256]{1,0:T(8,128)(2,1)S(1)} %collective-permute-done.29.refs_0_), channel_id=1, source_target_pairs={{0,24},{8,0},{16,8},{24,16},{1,25},{9,1},{17,9},{25,17},{2,26},{10... | collective-permute-start | bytes 2359304 | tf_op jit(solution)/shard_map/ppermute | solution.py:19
  35.3 11.7 %collective-permute-done.20.low.refs_1_ = bf16[1024,384]{1,0:T(8,128)(2,1)S(1)} collective-permute-done((bf16[1024,384]{1,0:T(8,128)(2,1)S(1)}, bf16[1024,384]{1,0:T(8,128)(2,1)S(1)}, u32[]{:S(2)}, u32[]{:S(2)}) %collective-permute-start.20) | collective-permute-done | bytes 786464 | tf_op jit(solution)/shard_map/ppermute | solution.py:19
  47.1 3.8 %collective-permute-start.28 = (bf16[1536,256]{1,0:T(8,128)(2,1)S(1)}, bf16[1536,256]{1,0:T(8,128)(2,1)S(1)}, u32[]{:S(2)}, u32[]{:S(2)}) collective-permute-start(bf16[1536,256]{1,0:T(8,128)(2,1)S(1)} %shard_map.54), channel_id=1, source_target_pairs={{0,8},{1,25},{8,16},{9,1},{16,24},{17,9},{24,0},{25,17},{2,10},{3,... | collective-permute-start | bytes 2359304 | tf_op jit(solution)/shard_map/ppermute | solution.py:71
  51.0 4.5 %collective-permute-done.low.refs_1_ = bf16[512,384]{1,0:T(8,128)(2,1)S(1)} collective-permute-done((bf16[512,384]{1,0:T(8,128)(2,1)S(1)}, bf16[512,384]{1,0:T(8,128)(2,1)S(1)}, u32[]{:S(2)}, u32[]{:S(2)}) %collective-permute-start) | collective-permute-done | bytes 393248 | tf_op jit(solution)/shard_map/ppermute | solution.py:19
  60.0 16.9 %collective-permute-done.1.upp.refs_2_ = bf16[512,384]{1,0:T(8,128)(2,1)S(1)} collective-permute-done((bf16[512,384]{1,0:T(8,128)(2,1)S(1)}, bf16[512,384]{1,0:T(8,128)(2,1)S(1)}, u32[]{:S(2)}, u32[]{:S(2)}) %collective-permute-start.1) | collective-permute-done | bytes 393248 | tf_op jit(solution)/shard_map/ppermute | solution.py:19
  78.6 2.1 %collective-permute-start.33 = (bf16[768,256]{1,0:T(8,128)(2,1)S(1)}, bf16[768,256]{1,0:T(8,128)(2,1)S(1)}, u32[]{:S(2)}, u32[]{:S(2)}) collective-permute-start(bf16[768,256]{1,0:T(8,128)(2,1)S(1)} %get-tuple-element.46), channel_id=1, source_target_pairs={{0,24},{8,0},{16,8},{24,16},{1,25},{9,1},{17,9},{25,17},{2,26},{10... | collective-permute-start | bytes 1179656 | tf_op jit(solution)/shard_map/ppermute | solution.py:19
  80.7 2.7 %collective-permute-done.8.upp.refs_2_ = bf16[512,384]{1,0:T(8,128)(2,1)S(1)} collective-permute-done((bf16[512,384]{1,0:T(8,128)(2,1)S(1)}, bf16[512,384]{1,0:T(8,128)(2,1)S(1)}, u32[]{:S(2)}, u32[]{:S(2)}) %collective-permute-start.8) | collective-permute-done | bytes 393248 | tf_op jit(solution)/shard_map/ppermute | solution.py:19
  83.5 2.5 %collective-permute-start.2 = (bf16[512,384]{1,0:T(8,128)(2,1)S(1)}, bf16[512,384]{1,0:T(8,128)(2,1)S(1)}, u32[]{:S(2)}, u32[]{:S(2)}) collective-permute-start(bf16[512,384]{1,0:T(8,128)(2,1)S(1)} %shard_map.37), channel_id=1, source_target_pairs={{0,32},{1,97},{32,64},{33,1},{64,96},{65,33},{96,0},{97,65},{2,34}... | collective-permute-start | bytes 1179656 | tf_op jit(solution)/shard_map/ppermute | solution.py:71
  87.6 2.1 %collective-permute-done.33.refs_4_ = bf16[768,256]{1,0:T(8,128)(2,1)S(1)} collective-permute-done((bf16[768,256]{1,0:T(8,128)(2,1)S(1)}, bf16[768,256]{1,0:T(8,128)(2,1)S(1)}, u32[]{:S(2)}, u32[]{:S(2)}) %collective-permute-start.33) | collective-permute-done | bytes 393248 | tf_op jit(solution)/shard_map/ppermute | solution.py:19
  93.2 2.0 %shard_map.60 = (f32[2,512,256]{2,1,0:T(8,128)S(1)}, f32[2,512,256]{2,1,0:T(8,128)S(1)}) custom-call(f32[2,512,512]{2,1,0:T(8,128)S(1)} %shard_map.59.s, bf16[512,1536]{1,0:T(8,128)(2,1)S(1)} %get-tuple-element.39.a, bf16[1536,256]{1,0:T(8,128)(2,1)S(1)} %collective-permute-done.29.refs_0_, bf16[1536,256]{1,0:T(8,128)(2,1)S(1)} %collective-permute-done.30.low.refs_1_, ...), custom_call_target="tpu_custom_call" | custom-call | tf_op jit(solution)/shard_map/pallas_call | solution.py:36
  95.2 2.7 %collective-permute-start.36 = (f32[2,512,256]{2,1,0:T(8,128)S(1)}, f32[2,512,256]{2,1,0:T(8,128)S(1)}, u32[]{:S(2)}, u32[]{:S(2)}) collective-permute-start(f32[2,512,256]{2,1,0:T(8,128)S(1)} %get-tuple-element.52), channel_id=1, source_target_pairs={{0,1},{1,0},{2,3},{3,2},{4,5},{5,4},{6,7},{7,6},{8,9},{9,8},{10,11... | collective-permute-start | bytes 3145736 | tf_op jit(solution)/shard_map/ppermute | solution.py:247
  102.1 2.7 %collective-permute-start.12 = (bf16[1536,128]{1,0:T(8,128)(2,1)S(1)}, bf16[1536,128]{1,0:T(8,128)(2,1)S(1)}, u32[]{:S(2)}, u32[]{:S(2)}) collective-permute-start(bf16[1536,128]{1,0:T(8,128)(2,1)S(1)} %collective-permute-done.10.refs_0_), channel_id=1, source_target_pairs={{0,24},{8,0},{16,8},{24,16},{1,25},{9,1},{17,9},{25,17},{2,26},{10... | collective-permute-start | bytes 1179656 | tf_op jit(solution)/shard_map/ppermute | solution.py:19
  104.8 8.7 %collective-permute-done.11.low.refs_1_ = bf16[1536,128]{1,0:T(8,128)(2,1)S(1)} collective-permute-done((bf16[1536,128]{1,0:T(8,128)(2,1)S(1)}, bf16[1536,128]{1,0:T(8,128)(2,1)S(1)}, u32[]{:S(2)}, u32[]{:S(2)}) %collective-permute-start.11) | collective-permute-done | bytes 393248 | tf_op jit(solution)/shard_map/ppermute | solution.py:19
  113.6 2.7 %collective-permute-start.14 = (bf16[768,128]{1,0:T(8,128)(2,1)S(1)}, bf16[768,128]{1,0:T(8,128)(2,1)S(1)}, u32[]{:S(2)}, u32[]{:S(2)}) collective-permute-start(bf16[768,128]{1,0:T(8,128)(2,1)S(1)} %get-tuple-element.33), channel_id=1, source_target_pairs={{0,24},{8,0},{16,8},{24,16},{1,25},{9,1},{17,9},{25,17},{2,26},{10... | collective-permute-start | bytes 589832 | tf_op jit(solution)/shard_map/ppermute | solution.py:19
  118.8 2.4 %collective-permute-done.13.refs_3_ = bf16[768,128]{1,0:T(8,128)(2,1)S(1)} collective-permute-done((bf16[768,128]{1,0:T(8,128)(2,1)S(1)}, bf16[768,128]{1,0:T(8,128)(2,1)S(1)}, u32[]{:S(2)}, u32[]{:S(2)}) %collective-permute-start.13) | collective-permute-done | bytes 196640 | tf_op jit(solution)/shard_map/ppermute | solution.py:19
  122.2 2.0 %collective-permute-start.15 = (f32[2,512,128]{2,1,0:T(8,128)S(1)}, f32[2,512,128]{2,1,0:T(8,128)S(1)}, u32[]{:S(2)}, u32[]{:S(2)}) collective-permute-start(f32[2,512,128]{2,1,0:T(8,128)S(1)} %get-tuple-element.35), channel_id=1, source_target_pairs={{0,1},{1,0},{2,3},{3,2},{4,5},{5,4},{6,7},{7,6},{8,9},{9,8},{10,11... | collective-permute-start | bytes 1572872 | tf_op jit(solution)/shard_map/ppermute | solution.py:247
  126.5 4.0 %collective-permute-done.16.bias_far = f32[12,128]{1,0:T(8,128)S(1)} collective-permute-done((f32[12,128]{1,0:T(8,128)S(1)}, f32[12,128]{1,0:T(8,128)S(1)}, u32[]{:S(2)}, u32[]{:S(2)}) %collective-permute-start.16) | collective-permute-done | bytes 6176 | tf_op jit(solution)/shard_map/ppermute | solution.py:26
  132.6 2.5 %collective-permute-start.38 = (bf16[512,256]{1,0:T(8,128)(2,1)S(1)}, bf16[512,256]{1,0:T(8,128)(2,1)S(1)}, u32[]{:S(2)}, u32[]{:S(2)}) collective-permute-start(bf16[512,256]{1,0:T(8,128)(2,1)S(1)} %get-tuple-element.54), channel_id=1, source_target_pairs={{0,6},{2,4},{4,2},{6,0},{1,7},{3,5},{5,3},{7,1},{8,14},{10,12},{12... | collective-permute-start | bytes 786440 | tf_op jit(solution)/shard_map/ppermute | solution.py:27
  137.2 2.0 %collective-permute-start.17 = (bf16[512,128]{1,0:T(8,128)(2,1)S(1)}, bf16[512,128]{1,0:T(8,128)(2,1)S(1)}, u32[]{:S(2)}, u32[]{:S(2)}) collective-permute-start(bf16[512,128]{1,0:T(8,128)(2,1)S(1)} %get-tuple-element.37), channel_id=1, source_target_pairs={{0,2},{2,0},{1,3},{3,1},{4,6},{6,4},{5,7},{7,5},{8,10},{10,8},{9,1... | collective-permute-start | bytes 393224 | tf_op jit(solution)/shard_map/ppermute | solution.py:26
  141.3 5.7 %collective-permute-done.38.refs_3_ = bf16[512,256]{1,0:T(8,128)(2,1)S(1)} collective-permute-done((bf16[512,256]{1,0:T(8,128)(2,1)S(1)}, bf16[512,256]{1,0:T(8,128)(2,1)S(1)}, u32[]{:S(2)}, u32[]{:S(2)}) %collective-permute-start.38) | collective-permute-done | bytes 262176 | tf_op jit(solution)/shard_map/ppermute | solution.py:27
  149.5 3.8 %collective-permute-done.25.refs_3_ = bf16[512,128]{1,0:T(8,128)(2,1)S(1)} collective-permute-done((bf16[512,128]{1,0:T(8,128)(2,1)S(1)}, bf16[512,128]{1,0:T(8,128)(2,1)S(1)}, u32[]{:S(2)}, u32[]{:S(2)}) %collective-permute-start.25) | collective-permute-done | bytes 131104 | tf_op jit(solution)/shard_map/ppermute | solution.py:27
  (85 shorter events, 42.6 us)
Async XLA Ops:
  2.1 26.4 %collective-permute-start.19 = (bf16[512,384]{1,0:T(8,128)(2,1)}, bf16[512,384]{1,0:T(8,128)(2,1)S(1)}, u32[]{:S(2)}, u32[]{:S(2)}) collective-permute-start(bf16[512,384]{1,0:T(8,128)(2,1)} %refs_0_.1), channel_id=1, source_target_pairs={{0,6},{2,4},{4,2},{6,0},{1,7},{3,5},{5,3},{7,1},{8,14},{10,12},{12... | collective-permute-start | bytes 1179656 | tf_op jit(solution)/shard_map/ppermute | solution.py:27
  5.4 25.9 %collective-permute-start.29 = (bf16[1536,256]{1,0:T(8,128)(2,1)S(1)}, bf16[1536,256]{1,0:T(8,128)(2,1)S(1)}, u32[]{:S(2)}, u32[]{:S(2)}) collective-permute-start(bf16[1536,256]{1,0:T(8,128)(2,1)S(1)} %get-tuple-element.44), channel_id=1, source_target_pairs={{0,2},{2,0},{1,3},{3,1},{4,6},{6,4},{5,7},{7,5},{8,10},{10,8},{9,1... | collective-permute-start | bytes 2359304 | tf_op jit(solution)/shard_map/ppermute | solution.py:26
  7.4 25.6 %collective-permute-start.26 = (bf16[1536,256]{1,0:T(8,128)(2,1)S(1)}, bf16[1536,256]{1,0:T(8,128)(2,1)S(1)}, u32[]{:S(2)}, u32[]{:S(2)}) collective-permute-start(bf16[1536,256]{1,0:T(8,128)(2,1)S(1)} %shard_map.53.refs_0_), channel_id=1, source_target_pairs={{0,8},{8,16},{16,24},{24,0},{1,9},{9,17},{17,25},{25,1},{2,10},{10... | collective-permute-start | bytes 2359304 | tf_op jit(solution)/shard_map/ppermute | solution.py:19
  9.1 26.1 %collective-permute-start.27 = (bf16[1536,256]{1,0:T(8,128)(2,1)S(1)}, bf16[1536,256]{1,0:T(8,128)(2,1)S(1)}, u32[]{:S(2)}, u32[]{:S(2)}) collective-permute-start(bf16[1536,256]{1,0:T(8,128)(2,1)S(1)} %shard_map.53.refs_0_), channel_id=1, source_target_pairs={{0,24},{8,0},{16,8},{24,16},{1,25},{9,1},{17,9},{25,17},{2,26},{10... | collective-permute-start | bytes 2359304 | tf_op jit(solution)/shard_map/ppermute | solution.py:19
  28.6 18.4 %collective-permute-start.20 = (bf16[1024,384]{1,0:T(8,128)(2,1)S(1)}, bf16[1024,384]{1,0:T(8,128)(2,1)S(1)}, u32[]{:S(2)}, u32[]{:S(2)}) collective-permute-start(bf16[1024,384]{1,0:T(8,128)(2,1)S(1)} %shard_map.47.refs_0_), channel_id=1, source_target_pairs={{0,32},{32,64},{64,96},{96,0},{1,33},{33,65},{65,97},{97,1},{2,34}... | collective-permute-start | bytes 2359304 | tf_op jit(solution)/shard_map/ppermute | solution.py:19
  29.9 17.2 %collective-permute-start.21 = (bf16[1024,384]{1,0:T(8,128)(2,1)S(1)}, bf16[1024,384]{1,0:T(8,128)(2,1)S(1)}, u32[]{:S(2)}, u32[]{:S(2)}) collective-permute-start(bf16[1024,384]{1,0:T(8,128)(2,1)S(1)} %shard_map.47.refs_0_), channel_id=1, source_target_pairs={{0,96},{32,0},{64,32},{96,64},{1,97},{33,1},{65,33},{97,65},{2,98}... | collective-permute-start | bytes 2359304 | tf_op jit(solution)/shard_map/ppermute | solution.py:19
  31.4 25.9 %collective-permute-start.30 = (bf16[1536,256]{1,0:T(8,128)(2,1)S(1)}, bf16[1536,256]{1,0:T(8,128)(2,1)S(1)}, u32[]{:S(2)}, u32[]{:S(2)}) collective-permute-start(bf16[1536,256]{1,0:T(8,128)(2,1)S(1)} %collective-permute-done.29.refs_0_), channel_id=1, source_target_pairs={{0,8},{8,16},{16,24},{24,0},{1,9},{9,17},{17,25},{25,1},{2,10},{10... | collective-permute-start | bytes 2359304 | tf_op jit(solution)/shard_map/ppermute | solution.py:19
  33.0 25.2 %collective-permute-start.31 = (bf16[1536,256]{1,0:T(8,128)(2,1)S(1)}, bf16[1536,256]{1,0:T(8,128)(2,1)S(1)}, u32[]{:S(2)}, u32[]{:S(2)}) collective-permute-start(bf16[1536,256]{1,0:T(8,128)(2,1)S(1)} %collective-permute-done.29.refs_0_), channel_id=1, source_target_pairs={{0,24},{8,0},{16,8},{24,16},{1,25},{9,1},{17,9},{25,17},{2,26},{10... | collective-permute-start | bytes 2359304 | tf_op jit(solution)/shard_map/ppermute | solution.py:19
  35.2 20.3 %collective-permute-start = (bf16[512,384]{1,0:T(8,128)(2,1)S(1)}, bf16[512,384]{1,0:T(8,128)(2,1)S(1)}, u32[]{:S(2)}, u32[]{:S(2)}) collective-permute-start(bf16[512,384]{1,0:T(8,128)(2,1)S(1)} %copy-done), channel_id=1, source_target_pairs={{0,32},{32,64},{64,96},{96,0},{1,33},{33,65},{65,97},{97,1},{2,34}... | collective-permute-start | bytes 1179656 | tf_op jit(solution)/shard_map/ppermute | solution.py:19
  47.1 38.9 %collective-permute-start.28 = (bf16[1536,256]{1,0:T(8,128)(2,1)S(1)}, bf16[1536,256]{1,0:T(8,128)(2,1)S(1)}, u32[]{:S(2)}, u32[]{:S(2)}) collective-permute-start(bf16[1536,256]{1,0:T(8,128)(2,1)S(1)} %shard_map.54), channel_id=1, source_target_pairs={{0,8},{1,25},{8,16},{9,1},{16,24},{17,9},{24,0},{25,17},{2,10},{3,... | collective-permute-start | bytes 2359304 | tf_op jit(solution)/shard_map/ppermute | solution.py:71
  55.5 30.6 %collective-permute-start.22 = (bf16[1024,384]{1,0:T(8,128)(2,1)S(1)}, bf16[1024,384]{1,0:T(8,128)(2,1)S(1)}, u32[]{:S(2)}, u32[]{:S(2)}) collective-permute-start(bf16[1024,384]{1,0:T(8,128)(2,1)S(1)} %shard_map.48), channel_id=1, source_target_pairs={{0,32},{1,97},{32,64},{33,1},{64,96},{65,33},{96,0},{97,65},{2,34}... | collective-permute-start | bytes 2359304 | tf_op jit(solution)/shard_map/ppermute | solution.py:71
  56.8 20.2 %collective-permute-start.1 = (bf16[512,384]{1,0:T(8,128)(2,1)S(1)}, bf16[512,384]{1,0:T(8,128)(2,1)S(1)}, u32[]{:S(2)}, u32[]{:S(2)}) collective-permute-start(bf16[512,384]{1,0:T(8,128)(2,1)S(1)} %copy-done), channel_id=1, source_target_pairs={{0,96},{32,0},{64,32},{96,64},{1,97},{33,1},{65,33},{97,65},{2,98}... | collective-permute-start | bytes 1179656 | tf_op jit(solution)/shard_map/ppermute | solution.py:19
  57.3 21.3 %collective-permute-start.7 = (bf16[512,384]{1,0:T(8,128)(2,1)S(1)}, bf16[512,384]{1,0:T(8,128)(2,1)S(1)}, u32[]{:S(2)}, u32[]{:S(2)}) collective-permute-start(bf16[512,384]{1,0:T(8,128)(2,1)S(1)} %collective-permute-done.6.refs_0_), channel_id=1, source_target_pairs={{0,32},{32,64},{64,96},{96,0},{1,33},{33,65},{65,97},{97,1},{2,34}... | collective-permute-start | bytes 1179656 | tf_op jit(solution)/shard_map/ppermute | solution.py:19
  58.2 25.2 %collective-permute-start.8 = (bf16[512,384]{1,0:T(8,128)(2,1)S(1)}, bf16[512,384]{1,0:T(8,128)(2,1)S(1)}, u32[]{:S(2)}, u32[]{:S(2)}) collective-permute-start(bf16[512,384]{1,0:T(8,128)(2,1)S(1)} %collective-permute-done.6.refs_0_), channel_id=1, source_target_pairs={{0,96},{32,0},{64,32},{96,64},{1,97},{33,1},{65,33},{97,65},{2,98}... | collective-permute-start | bytes 1179656 | tf_op jit(solution)/shard_map/ppermute | solution.py:19
  86.1 15.9 %collective-permute-start.10 = (bf16[1536,128]{1,0:T(8,128)(2,1)S(1)}, bf16[1536,128]{1,0:T(8,128)(2,1)S(1)}, u32[]{:S(2)}, u32[]{:S(2)}) collective-permute-start(bf16[1536,128]{1,0:T(8,128)(2,1)S(1)} %get-tuple-element.31), channel_id=1, source_target_pairs={{0,2},{2,0},{1,3},{3,1},{4,6},{6,4},{5,7},{7,5},{8,10},{10,8},{9,1... | collective-permute-start | bytes 1179656 | tf_op jit(solution)/shard_map/ppermute | solution.py:26
  87.2 14.9 %collective-permute-start.3 = (bf16[1536,128]{1,0:T(8,128)(2,1)S(1)}, bf16[1536,128]{1,0:T(8,128)(2,1)S(1)}, u32[]{:S(2)}, u32[]{:S(2)}) collective-permute-start(bf16[1536,128]{1,0:T(8,128)(2,1)S(1)} %get-tuple-element.30.refs_0_), channel_id=1, source_target_pairs={{0,8},{8,16},{16,24},{24,0},{1,9},{9,17},{17,25},{25,1},{2,10},{10... | collective-permute-start | bytes 1179656 | tf_op jit(solution)/shard_map/ppermute | solution.py:19
  89.7 15.0 %collective-permute-start.4 = (bf16[1536,128]{1,0:T(8,128)(2,1)S(1)}, bf16[1536,128]{1,0:T(8,128)(2,1)S(1)}, u32[]{:S(2)}, u32[]{:S(2)}) collective-permute-start(bf16[1536,128]{1,0:T(8,128)(2,1)S(1)} %get-tuple-element.30.refs_0_), channel_id=1, source_target_pairs={{0,24},{8,0},{16,8},{24,16},{1,25},{9,1},{17,9},{25,17},{2,26},{10... | collective-permute-start | bytes 1179656 | tf_op jit(solution)/shard_map/ppermute | solution.py:19
  95.2 35.3 %collective-permute-start.36 = (f32[2,512,256]{2,1,0:T(8,128)S(1)}, f32[2,512,256]{2,1,0:T(8,128)S(1)}, u32[]{:S(2)}, u32[]{:S(2)}) collective-permute-start(f32[2,512,256]{2,1,0:T(8,128)S(1)} %get-tuple-element.52), channel_id=1, source_target_pairs={{0,1},{1,0},{2,3},{3,2},{4,5},{5,4},{6,7},{7,6},{8,9},{9,8},{10,11... | collective-permute-start | bytes 3145736 | tf_op jit(solution)/shard_map/ppermute | solution.py:247
  101.9 33.3 %collective-permute-start.34 = (f32[2,512,256]{2,1,0:T(8,128)S(1)}, f32[2,512,256]{2,1,0:T(8,128)S(1)}, u32[]{:S(2)}, u32[]{:S(2)}) collective-permute-start(f32[2,512,256]{2,1,0:T(8,128)S(1)} %get-tuple-element.48), channel_id=1, source_target_pairs={{0,1},{1,0},{2,3},{3,2},{4,5},{5,4},{6,7},{7,6},{8,9},{9,8},{10,11... | collective-permute-start | bytes 3145736 | tf_op jit(solution)/shard_map/ppermute | solution.py:247
  104.7 13.1 %collective-permute-start.5 = (bf16[1536,128]{1,0:T(8,128)(2,1)S(1)}, bf16[1536,128]{1,0:T(8,128)(2,1)S(1)}, u32[]{:S(2)}, u32[]{:S(2)}) collective-permute-start(bf16[1536,128]{1,0:T(8,128)(2,1)S(1)} %shard_map.40), channel_id=1, source_target_pairs={{0,8},{1,25},{8,16},{9,1},{16,24},{17,9},{24,0},{25,17},{2,10},{3,... | collective-permute-start | bytes 1179656 | tf_op jit(solution)/shard_map/ppermute | solution.py:71
  122.2 14.6 %collective-permute-start.15 = (f32[2,512,128]{2,1,0:T(8,128)S(1)}, f32[2,512,128]{2,1,0:T(8,128)S(1)}, u32[]{:S(2)}, u32[]{:S(2)}) collective-permute-start(f32[2,512,128]{2,1,0:T(8,128)S(1)} %get-tuple-element.35), channel_id=1, source_target_pairs={{0,1},{1,0},{2,3},{3,2},{4,5},{5,4},{6,7},{7,6},{8,9},{9,8},{10,11... | collective-permute-start | bytes 1572872 | tf_op jit(solution)/shard_map/ppermute | solution.py:247
  126.3 12.9 %collective-permute-start.23 = (f32[2,512,128]{2,1,0:T(8,128)S(1)}, f32[2,512,128]{2,1,0:T(8,128)S(1)}, u32[]{:S(2)}, u32[]{:S(2)}) collective-permute-start(f32[2,512,128]{2,1,0:T(8,128)S(1)} %get-tuple-element.41), channel_id=1, source_target_pairs={{0,1},{1,0},{2,3},{3,2},{4,5},{5,4},{6,7},{7,6},{8,9},{9,8},{10,11... | collective-permute-start | bytes 1572872 | tf_op jit(solution)/shard_map/ppermute | solution.py:247
  132.6 14.4 %collective-permute-start.38 = (bf16[512,256]{1,0:T(8,128)(2,1)S(1)}, bf16[512,256]{1,0:T(8,128)(2,1)S(1)}, u32[]{:S(2)}, u32[]{:S(2)}) collective-permute-start(bf16[512,256]{1,0:T(8,128)(2,1)S(1)} %get-tuple-element.54), channel_id=1, source_target_pairs={{0,6},{2,4},{4,2},{6,0},{1,7},{3,5},{5,3},{7,1},{8,14},{10,12},{12... | collective-permute-start | bytes 786440 | tf_op jit(solution)/shard_map/ppermute | solution.py:27
  140.3 13.0 %collective-permute-start.25 = (bf16[512,128]{1,0:T(8,128)(2,1)S(1)}, bf16[512,128]{1,0:T(8,128)(2,1)S(1)}, u32[]{:S(2)}, u32[]{:S(2)}) collective-permute-start(bf16[512,128]{1,0:T(8,128)(2,1)S(1)} %get-tuple-element.43), channel_id=1, source_target_pairs={{0,6},{2,4},{4,2},{6,0},{1,7},{3,5},{5,3},{7,1},{8,14},{10,12},{12... | collective-permute-start | bytes 393224 | tf_op jit(solution)/shard_map/ppermute | solution.py:27
  (17 other events, 182.4 us)

commit v2 on v1

--- a/solution.py
+++ b/solution.py
@@ -142,33 +142,30 @@
     return call(body, vmem((2, 512, 2 * width), jnp.float32), [rows, *blocks])
 
 
-def far_sums(sums, rows, blocks, chunk):
+def far_sums(sums, rows, blocks, chunk, keep):
     near, offset, width = chunk
     apart = NEAR[near][1]
 
     def body(s, a, *refs):
-        blocks, keep, send = refs[:-2], refs[-2], refs[-1]
+        blocks, out = refs[:-1], refs[-1]
         _, z, _, b, c = places()
         even, odd = sides(*blocks)
 
-        def fill(parity, side, owner, target):
+        def fill(parity, side, owner):
             first = ((owner % 4) // 2 + b) % 2
             total = jnp.dot(a[...], side(), preferred_element_type=jnp.float32)
-            target[first] = total[:, :width] + s[parity, :, offset : offset + width]
-            target[1 - first] = total[:, width:] + s[parity, :, apart + offset : apart + offset + width]
-
-        @pl.when(z % 2 == c)
+            out[first] = total[:, :width] + s[parity, :, offset : offset + width]
+            out[1 - first] = total[:, width:] + s[parity, :, apart + offset : apart + offset + width]
+
+        @pl.when((z % 2 == c) == keep)
         def _():
-            fill(1, odd, z + 3, send)
-            fill(0, even, z, keep)
-
-        @pl.when(z % 2 != c)
+            fill(0, even, z)
+
+        @pl.when((z % 2 == c) != keep)
         def _():
-            fill(0, even, z, send)
-            fill(1, odd, z + 3, keep)
-
-    shape = vmem((2, 512, width), jnp.float32)
-    return call(body, (shape, shape), [sums, rows, *blocks])
+            fill(1, odd, z + 3)
+
+    return call(body, vmem((2, 512, width), jnp.float32), [sums, rows, *blocks])
 
 
 def activate(keep, other, mine, theirs, chunk):
@@ -243,8 +240,9 @@
     for k, chunk in enumerate(FAR):
         blocks = {}
         for ra, rows in ((1, far_across), (0, far_own)):
-            keep, send = far_sums(sums[chunk[0], ra], rows, far[k], chunk)
-            other = lax.ppermute(send, "c", SWAP)
+            of = sums[chunk[0], ra], rows, far[k], chunk
+            other = lax.ppermute(far_sums(*of, False), "c", SWAP)
+            keep = far_sums(*of, True)
             blocks[ra] = activate(keep, other, bias, theirs, chunk)
         pieces = [blocks[0][0], across(blocks[0][1], 1), across(blocks[1][0], 2), across(blocks[1][1], 3)]
         hidden = lay_out(pieces, chunk, hidden)

time: 154 us -> 153 us (level)
  waiting for transfers between devices: 83.8 us -> 81.7 us
    ppermute x6, waiting for transfers between devices: 5.51 us -> 3 us  [across(): return lax.ppermute(v, 'b', SWAP)]
    pallas_call x27 -> x31, Pallas kernels: 18.4 us -> 18.9 us  [call(): pl.pallas_call(body, out_shape=outs, in_specs=[VMEM] * len(args) + [ANY]...]
  transfers between devices with their start and end apart: 39 -> 39, of which waited for: 14 -> 13; matrix products, arithmetic and copies ran while one was open for 0% -> 0% of each run, Pallas kernels for 11% -> 12%
where the time goes in v2:
time: 153 us
  waiting for transfers between devices  81.7 us (53%)
  starting transfers between devices  51.8 us (34%)
  Pallas kernels  18.9 us (12%)
    ppermute x18, waiting for transfers between devices, shift(): return lax.ppermute(v, axis, [(i, (i + step) % 4) for i in range(4)])  49.7 us
    ppermute x3, waiting for transfers between devices, across(): return lax.ppermute(v, ('a', 'b'), [(i, i ^ 3) for i in range(4)])  27.4 us
    ppermute x18, starting transfers between devices, shift(): return lax.ppermute(v, axis, [(i, (i + step) % 4) for i in range(4)])  24.8 us
    pallas_call x31, Pallas kernels, call(): pl.pallas_call(body, out_shape=outs, in_specs=[VMEM] * len(args) + [ANY]...  18.9 us
    ppermute x5, starting transfers between devices, ring_gather(): return (block, lower, upper, lax.ppermute(chosen, (axis, 'c'), pairs))  8.07 us
    ppermute x4, starting transfers between devices, per_device_in_order(): other = lax.ppermute(far_sums(*of, False), 'c', SWAP)  5.14 us
    ppermute x3, starting transfers between devices, across(): return lax.ppermute(v, ('a', 'b'), [(i, i ^ 3) for i in range(4)])  5.04 us
    ppermute x3, starting transfers between devices, across(): return lax.ppermute(v, 'a', SWAP)  4.59 us
  transfers between devices with their start and end apart: 39, of which 13 were waited for; matrix products, arithmetic and copies ran while one was open for 0% of the time, Pallas kernels for 12%

profile of v2, /device:TPU:1, one launch (start us, length us, event | category | flops | bytes accessed | tf_op | source)
XLA Modules:
  0.0 152.9 jit_solution(15246505127967891395)
XLA Ops:
  0.0 2.1 %collective-permute-start.18 = (bf16[512,384]{1,0:T(8,128)(2,1)}, bf16[512,384]{1,0:T(8,128)(2,1)S(1)}, u32[]{:S(2)}, u32[]{:S(2)}) collective-permute-start(bf16[512,384]{1,0:T(8,128)(2,1)} %refs_0_.1), channel_id=1, source_target_pairs={{0,4},{4,0},{1,5},{5,1},{2,6},{6,2},{3,7},{7,3},{8,12},{12,8},{9,1... | collective-permute-start | bytes 1179656 | tf_op jit(solution)/shard_map/ppermute | solution.py:24
  2.1 1.9 %collective-permute-start.19 = (bf16[512,384]{1,0:T(8,128)(2,1)}, bf16[512,384]{1,0:T(8,128)(2,1)S(1)}, u32[]{:S(2)}, u32[]{:S(2)}) collective-permute-start(bf16[512,384]{1,0:T(8,128)(2,1)} %refs_0_.1), channel_id=1, source_target_pairs={{0,6},{2,4},{4,2},{6,0},{1,7},{3,5},{5,3},{7,1},{8,14},{10,12},{12... | collective-permute-start | bytes 1179656 | tf_op jit(solution)/shard_map/ppermute | solution.py:27
  9.1 2.2 %collective-permute-start.27 = (bf16[1536,256]{1,0:T(8,128)(2,1)S(1)}, bf16[1536,256]{1,0:T(8,128)(2,1)S(1)}, u32[]{:S(2)}, u32[]{:S(2)}) collective-permute-start(bf16[1536,256]{1,0:T(8,128)(2,1)S(1)} %shard_map.55.refs_0_), channel_id=1, source_target_pairs={{0,24},{8,0},{16,8},{24,16},{1,25},{9,1},{17,9},{25,17},{2,26},{10... | collective-permute-start | bytes 2359304 | tf_op jit(solution)/shard_map/ppermute | solution.py:19
  11.3 17.3 %collective-permute-done.19.refs_1_ = bf16[512,384]{1,0:T(8,128)(2,1)S(1)} collective-permute-done((bf16[512,384]{1,0:T(8,128)(2,1)}, bf16[512,384]{1,0:T(8,128)(2,1)S(1)}, u32[]{:S(2)}, u32[]{:S(2)}) %collective-permute-start.19) | collective-permute-done | bytes 393248 | tf_op jit(solution)/shard_map/ppermute | solution.py:27
  33.0 2.2 %collective-permute-start.31 = (bf16[1536,256]{1,0:T(8,128)(2,1)S(1)}, bf16[1536,256]{1,0:T(8,128)(2,1)S(1)}, u32[]{:S(2)}, u32[]{:S(2)}) collective-permute-start(bf16[1536,256]{1,0:T(8,128)(2,1)S(1)} %collective-permute-done.29.refs_0_), channel_id=1, source_target_pairs={{0,24},{8,0},{16,8},{24,16},{1,25},{9,1},{17,9},{25,17},{2,26},{10... | collective-permute-start | bytes 2359304 | tf_op jit(solution)/shard_map/ppermute | solution.py:19
  35.3 11.7 %collective-permute-done.20.low.refs_1_ = bf16[1024,384]{1,0:T(8,128)(2,1)S(1)} collective-permute-done((bf16[1024,384]{1,0:T(8,128)(2,1)S(1)}, bf16[1024,384]{1,0:T(8,128)(2,1)S(1)}, u32[]{:S(2)}, u32[]{:S(2)}) %collective-permute-start.20) | collective-permute-done | bytes 786464 | tf_op jit(solution)/shard_map/ppermute | solution.py:19
  47.1 3.8 %collective-permute-start.28 = (bf16[1536,256]{1,0:T(8,128)(2,1)S(1)}, bf16[1536,256]{1,0:T(8,128)(2,1)S(1)}, u32[]{:S(2)}, u32[]{:S(2)}) collective-permute-start(bf16[1536,256]{1,0:T(8,128)(2,1)S(1)} %shard_map.56), channel_id=1, source_target_pairs={{0,8},{1,25},{8,16},{9,1},{16,24},{17,9},{24,0},{25,17},{2,10},{3,... | collective-permute-start | bytes 2359304 | tf_op jit(solution)/shard_map/ppermute | solution.py:71
  51.0 4.5 %collective-permute-done.low.refs_1_ = bf16[512,384]{1,0:T(8,128)(2,1)S(1)} collective-permute-done((bf16[512,384]{1,0:T(8,128)(2,1)S(1)}, bf16[512,384]{1,0:T(8,128)(2,1)S(1)}, u32[]{:S(2)}, u32[]{:S(2)}) %collective-permute-start) | collective-permute-done | bytes 393248 | tf_op jit(solution)/shard_map/ppermute | solution.py:19
  60.0 16.9 %collective-permute-done.1.upp.refs_2_ = bf16[512,384]{1,0:T(8,128)(2,1)S(1)} collective-permute-done((bf16[512,384]{1,0:T(8,128)(2,1)S(1)}, bf16[512,384]{1,0:T(8,128)(2,1)S(1)}, u32[]{:S(2)}, u32[]{:S(2)}) %collective-permute-start.1) | collective-permute-done | bytes 393248 | tf_op jit(solution)/shard_map/ppermute | solution.py:19
  78.6 2.1 %collective-permute-start.33 = (bf16[768,256]{1,0:T(8,128)(2,1)S(1)}, bf16[768,256]{1,0:T(8,128)(2,1)S(1)}, u32[]{:S(2)}, u32[]{:S(2)}) collective-permute-start(bf16[768,256]{1,0:T(8,128)(2,1)S(1)} %get-tuple-element.34), channel_id=1, source_target_pairs={{0,24},{8,0},{16,8},{24,16},{1,25},{9,1},{17,9},{25,17},{2,26},{10... | collective-permute-start | bytes 1179656 | tf_op jit(solution)/shard_map/ppermute | solution.py:19
  80.7 2.7 %collective-permute-done.8.upp.refs_2_ = bf16[512,384]{1,0:T(8,128)(2,1)S(1)} collective-permute-done((bf16[512,384]{1,0:T(8,128)(2,1)S(1)}, bf16[512,384]{1,0:T(8,128)(2,1)S(1)}, u32[]{:S(2)}, u32[]{:S(2)}) %collective-permute-start.8) | collective-permute-done | bytes 393248 | tf_op jit(solution)/shard_map/ppermute | solution.py:19
  83.5 2.5 %collective-permute-start.2 = (bf16[512,384]{1,0:T(8,128)(2,1)S(1)}, bf16[512,384]{1,0:T(8,128)(2,1)S(1)}, u32[]{:S(2)}, u32[]{:S(2)}) collective-permute-start(bf16[512,384]{1,0:T(8,128)(2,1)S(1)} %shard_map.37), channel_id=1, source_target_pairs={{0,32},{1,97},{32,64},{33,1},{64,96},{65,33},{96,0},{97,65},{2,34}... | collective-permute-start | bytes 1179656 | tf_op jit(solution)/shard_map/ppermute | solution.py:71
  87.6 2.1 %collective-permute-done.33.refs_4_ = bf16[768,256]{1,0:T(8,128)(2,1)S(1)} collective-permute-done((bf16[768,256]{1,0:T(8,128)(2,1)S(1)}, bf16[768,256]{1,0:T(8,128)(2,1)S(1)}, u32[]{:S(2)}, u32[]{:S(2)}) %collective-permute-start.33) | collective-permute-done | bytes 393248 | tf_op jit(solution)/shard_map/ppermute | solution.py:19
  94.2 2.9 %collective-permute-start.36 = (f32[2,512,256]{2,1,0:T(8,128)S(1)}, f32[2,512,256]{2,1,0:T(8,128)S(1)}, u32[]{:S(2)}, u32[]{:S(2)}) collective-permute-start(f32[2,512,256]{2,1,0:T(8,128)S(1)} %shard_map.64), channel_id=1, source_target_pairs={{0,1},{1,0},{2,3},{3,2},{4,5},{5,4},{6,7},{7,6},{8,9},{9,8},{10,11... | collective-permute-start | bytes 3145736 | tf_op jit(solution)/shard_map/ppermute | solution.py:244
  100.4 2.7 %collective-permute-start.12 = (bf16[1536,128]{1,0:T(8,128)(2,1)S(1)}, bf16[1536,128]{1,0:T(8,128)(2,1)S(1)}, u32[]{:S(2)}, u32[]{:S(2)}) collective-permute-start(bf16[1536,128]{1,0:T(8,128)(2,1)S(1)} %collective-permute-done.10.refs_0_), channel_id=1, source_target_pairs={{0,24},{8,0},{16,8},{24,16},{1,25},{9,1},{17,9},{25,17},{2,26},{10... | collective-permute-start | bytes 1179656 | tf_op jit(solution)/shard_map/ppermute | solution.py:19
  103.6 8.3 %collective-permute-done.11.low.refs_1_ = bf16[1536,128]{1,0:T(8,128)(2,1)S(1)} collective-permute-done((bf16[1536,128]{1,0:T(8,128)(2,1)S(1)}, bf16[1536,128]{1,0:T(8,128)(2,1)S(1)}, u32[]{:S(2)}, u32[]{:S(2)}) %collective-permute-start.11) | collective-permute-done | bytes 393248 | tf_op jit(solution)/shard_map/ppermute | solution.py:19
  112.0 2.7 %collective-permute-start.14 = (bf16[768,128]{1,0:T(8,128)(2,1)S(1)}, bf16[768,128]{1,0:T(8,128)(2,1)S(1)}, u32[]{:S(2)}, u32[]{:S(2)}) collective-permute-start(bf16[768,128]{1,0:T(8,128)(2,1)S(1)} %get-tuple-element.25), channel_id=1, source_target_pairs={{0,24},{8,0},{16,8},{24,16},{1,25},{9,1},{17,9},{25,17},{2,26},{10... | collective-permute-start | bytes 589832 | tf_op jit(solution)/shard_map/ppermute | solution.py:19
  117.2 2.4 %collective-permute-done.13.refs_3_ = bf16[768,128]{1,0:T(8,128)(2,1)S(1)} collective-permute-done((bf16[768,128]{1,0:T(8,128)(2,1)S(1)}, bf16[768,128]{1,0:T(8,128)(2,1)S(1)}, u32[]{:S(2)}, u32[]{:S(2)}) %collective-permute-start.13) | collective-permute-done | bytes 196640 | tf_op jit(solution)/shard_map/ppermute | solution.py:19
  120.2 2.0 %collective-permute-start.15 = (f32[2,512,128]{2,1,0:T(8,128)S(1)}, f32[2,512,128]{2,1,0:T(8,128)S(1)}, u32[]{:S(2)}, u32[]{:S(2)}) collective-permute-start(f32[2,512,128]{2,1,0:T(8,128)S(1)} %shard_map.46), channel_id=1, source_target_pairs={{0,1},{1,0},{2,3},{3,2},{4,5},{5,4},{6,7},{7,6},{8,9},{9,8},{10,11... | collective-permute-start | bytes 1572872 | tf_op jit(solution)/shard_map/ppermute | solution.py:244
  125.0 3.0 %collective-permute-done.16.bias_far = f32[12,128]{1,0:T(8,128)S(1)} collective-permute-done((f32[12,128]{1,0:T(8,128)S(1)}, f32[12,128]{1,0:T(8,128)S(1)}, u32[]{:S(2)}, u32[]{:S(2)}) %collective-permute-start.16) | collective-permute-done | bytes 6176 | tf_op jit(solution)/shard_map/ppermute | solution.py:26
  131.2 2.5 %collective-permute-start.38 = (bf16[512,256]{1,0:T(8,128)(2,1)S(1)}, bf16[512,256]{1,0:T(8,128)(2,1)S(1)}, u32[]{:S(2)}, u32[]{:S(2)}) collective-permute-start(bf16[512,256]{1,0:T(8,128)(2,1)S(1)} %get-tuple-element.38), channel_id=1, source_target_pairs={{0,6},{2,4},{4,2},{6,0},{1,7},{3,5},{5,3},{7,1},{8,14},{10,12},{12... | collective-permute-start | bytes 786440 | tf_op jit(solution)/shard_map/ppermute | solution.py:27
  136.4 1.9 %collective-permute-start.17 = (bf16[512,128]{1,0:T(8,128)(2,1)S(1)}, bf16[512,128]{1,0:T(8,128)(2,1)S(1)}, u32[]{:S(2)}, u32[]{:S(2)}) collective-permute-start(bf16[512,128]{1,0:T(8,128)(2,1)S(1)} %get-tuple-element.27), channel_id=1, source_target_pairs={{0,2},{2,0},{1,3},{3,1},{4,6},{6,4},{5,7},{7,5},{8,10},{10,8},{9,1... | collective-permute-start | bytes 393224 | tf_op jit(solution)/shard_map/ppermute | solution.py:26
  140.7 5.7 %collective-permute-done.38.refs_3_ = bf16[512,256]{1,0:T(8,128)(2,1)S(1)} collective-permute-done((bf16[512,256]{1,0:T(8,128)(2,1)S(1)}, bf16[512,256]{1,0:T(8,128)(2,1)S(1)}, u32[]{:S(2)}, u32[]{:S(2)}) %collective-permute-start.38) | collective-permute-done | bytes 262176 | tf_op jit(solution)/shard_map/ppermute | solution.py:27
  147.5 4.5 %collective-permute-done.25.refs_3_ = bf16[512,128]{1,0:T(8,128)(2,1)S(1)} collective-permute-done((bf16[512,128]{1,0:T(8,128)(2,1)S(1)}, bf16[512,128]{1,0:T(8,128)(2,1)S(1)}, u32[]{:S(2)}, u32[]{:S(2)}) %collective-permute-start.25) | collective-permute-done | bytes 131104 | tf_op jit(solution)/shard_map/ppermute | solution.py:27
  (89 shorter events, 41.9 us)
Async XLA Ops:
  2.1 26.4 %collective-permute-start.19 = (bf16[512,384]{1,0:T(8,128)(2,1)}, bf16[512,384]{1,0:T(8,128)(2,1)S(1)}, u32[]{:S(2)}, u32[]{:S(2)}) collective-permute-start(bf16[512,384]{1,0:T(8,128)(2,1)} %refs_0_.1), channel_id=1, source_target_pairs={{0,6},{2,4},{4,2},{6,0},{1,7},{3,5},{5,3},{7,1},{8,14},{10,12},{12... | collective-permute-start | bytes 1179656 | tf_op jit(solution)/shard_map/ppermute | solution.py:27
  5.4 25.9 %collective-permute-start.29 = (bf16[1536,256]{1,0:T(8,128)(2,1)S(1)}, bf16[1536,256]{1,0:T(8,128)(2,1)S(1)}, u32[]{:S(2)}, u32[]{:S(2)}) collective-permute-start(bf16[1536,256]{1,0:T(8,128)(2,1)S(1)} %get-tuple-element.32), channel_id=1, source_target_pairs={{0,2},{2,0},{1,3},{3,1},{4,6},{6,4},{5,7},{7,5},{8,10},{10,8},{9,1... | collective-permute-start | bytes 2359304 | tf_op jit(solution)/shard_map/ppermute | solution.py:26
  7.4 25.6 %collective-permute-start.26 = (bf16[1536,256]{1,0:T(8,128)(2,1)S(1)}, bf16[1536,256]{1,0:T(8,128)(2,1)S(1)}, u32[]{:S(2)}, u32[]{:S(2)}) collective-permute-start(bf16[1536,256]{1,0:T(8,128)(2,1)S(1)} %shard_map.55.refs_0_), channel_id=1, source_target_pairs={{0,8},{8,16},{16,24},{24,0},{1,9},{9,17},{17,25},{25,1},{2,10},{10... | collective-permute-start | bytes 2359304 | tf_op jit(solution)/shard_map/ppermute | solution.py:19
  9.1 26.1 %collective-permute-start.27 = (bf16[1536,256]{1,0:T(8,128)(2,1)S(1)}, bf16[1536,256]{1,0:T(8,128)(2,1)S(1)}, u32[]{:S(2)}, u32[]{:S(2)}) collective-permute-start(bf16[1536,256]{1,0:T(8,128)(2,1)S(1)} %shard_map.55.refs_0_), channel_id=1, source_target_pairs={{0,24},{8,0},{16,8},{24,16},{1,25},{9,1},{17,9},{25,17},{2,26},{10... | collective-permute-start | bytes 2359304 | tf_op jit(solution)/shard_map/ppermute | solution.py:19
  28.6 18.4 %collective-permute-start.20 = (bf16[1024,384]{1,0:T(8,128)(2,1)S(1)}, bf16[1024,384]{1,0:T(8,128)(2,1)S(1)}, u32[]{:S(2)}, u32[]{:S(2)}) collective-permute-start(bf16[1024,384]{1,0:T(8,128)(2,1)S(1)} %shard_map.48.refs_0_), channel_id=1, source_target_pairs={{0,32},{32,64},{64,96},{96,0},{1,33},{33,65},{65,97},{97,1},{2,34}... | collective-permute-start | bytes 2359304 | tf_op jit(solution)/shard_map/ppermute | solution.py:19
  29.9 17.2 %collective-permute-start.21 = (bf16[1024,384]{1,0:T(8,128)(2,1)S(1)}, bf16[1024,384]{1,0:T(8,128)(2,1)S(1)}, u32[]{:S(2)}, u32[]{:S(2)}) collective-permute-start(bf16[1024,384]{1,0:T(8,128)(2,1)S(1)} %shard_map.48.refs_0_), channel_id=1, source_target_pairs={{0,96},{32,0},{64,32},{96,64},{1,97},{33,1},{65,33},{97,65},{2,98}... | collective-permute-start | bytes 2359304 | tf_op jit(solution)/shard_map/ppermute | solution.py:19
  31.4 25.9 %collective-permute-start.30 = (bf16[1536,256]{1,0:T(8,128)(2,1)S(1)}, bf16[1536,256]{1,0:T(8,128)(2,1)S(1)}, u32[]{:S(2)}, u32[]{:S(2)}) collective-permute-start(bf16[1536,256]{1,0:T(8,128)(2,1)S(1)} %collective-permute-done.29.refs_0_), channel_id=1, source_target_pairs={{0,8},{8,16},{16,24},{24,0},{1,9},{9,17},{17,25},{25,1},{2,10},{10... | collective-permute-start | bytes 2359304 | tf_op jit(solution)/shard_map/ppermute | solution.py:19
  33.0 25.2 %collective-permute-start.31 = (bf16[1536,256]{1,0:T(8,128)(2,1)S(1)}, bf16[1536,256]{1,0:T(8,128)(2,1)S(1)}, u32[]{:S(2)}, u32[]{:S(2)}) collective-permute-start(bf16[1536,256]{1,0:T(8,128)(2,1)S(1)} %collective-permute-done.29.refs_0_), channel_id=1, source_target_pairs={{0,24},{8,0},{16,8},{24,16},{1,25},{9,1},{17,9},{25,17},{2,26},{10... | collective-permute-start | bytes 2359304 | tf_op jit(solution)/shard_map/ppermute | solution.py:19
  35.2 20.3 %collective-permute-start = (bf16[512,384]{1,0:T(8,128)(2,1)S(1)}, bf16[512,384]{1,0:T(8,128)(2,1)S(1)}, u32[]{:S(2)}, u32[]{:S(2)}) collective-permute-start(bf16[512,384]{1,0:T(8,128)(2,1)S(1)} %copy-done), channel_id=1, source_target_pairs={{0,32},{32,64},{64,96},{96,0},{1,33},{33,65},{65,97},{97,1},{2,34}... | collective-permute-start | bytes 1179656 | tf_op jit(solution)/shard_map/ppermute | solution.py:19
  47.1 38.9 %collective-permute-start.28 = (bf16[1536,256]{1,0:T(8,128)(2,1)S(1)}, bf16[1536,256]{1,0:T(8,128)(2,1)S(1)}, u32[]{:S(2)}, u32[]{:S(2)}) collective-permute-start(bf16[1536,256]{1,0:T(8,128)(2,1)S(1)} %shard_map.56), channel_id=1, source_target_pairs={{0,8},{1,25},{8,16},{9,1},{16,24},{17,9},{24,0},{25,17},{2,10},{3,... | collective-permute-start | bytes 2359304 | tf_op jit(solution)/shard_map/ppermute | solution.py:71
  55.5 30.6 %collective-permute-start.22 = (bf16[1024,384]{1,0:T(8,128)(2,1)S(1)}, bf16[1024,384]{1,0:T(8,128)(2,1)S(1)}, u32[]{:S(2)}, u32[]{:S(2)}) collective-permute-start(bf16[1024,384]{1,0:T(8,128)(2,1)S(1)} %shard_map.49), channel_id=1, source_target_pairs={{0,32},{1,97},{32,64},{33,1},{64,96},{65,33},{96,0},{97,65},{2,34}... | collective-permute-start | bytes 2359304 | tf_op jit(solution)/shard_map/ppermute | solution.py:71
  56.8 20.2 %collective-permute-start.1 = (bf16[512,384]{1,0:T(8,128)(2,1)S(1)}, bf16[512,384]{1,0:T(8,128)(2,1)S(1)}, u32[]{:S(2)}, u32[]{:S(2)}) collective-permute-start(bf16[512,384]{1,0:T(8,128)(2,1)S(1)} %copy-done), channel_id=1, source_target_pairs={{0,96},{32,0},{64,32},{96,64},{1,97},{33,1},{65,33},{97,65},{2,98}... | collective-permute-start | bytes 1179656 | tf_op jit(solution)/shard_map/ppermute | solution.py:19
  57.3 21.3 %collective-permute-start.7 = (bf16[512,384]{1,0:T(8,128)(2,1)S(1)}, bf16[512,384]{1,0:T(8,128)(2,1)S(1)}, u32[]{:S(2)}, u32[]{:S(2)}) collective-permute-start(bf16[512,384]{1,0:T(8,128)(2,1)S(1)} %collective-permute-done.6.refs_0_), channel_id=1, source_target_pairs={{0,32},{32,64},{64,96},{96,0},{1,33},{33,65},{65,97},{97,1},{2,34}... | collective-permute-start | bytes 1179656 | tf_op jit(solution)/shard_map/ppermute | solution.py:19
  58.2 25.2 %collective-permute-start.8 = (bf16[512,384]{1,0:T(8,128)(2,1)S(1)}, bf16[512,384]{1,0:T(8,128)(2,1)S(1)}, u32[]{:S(2)}, u32[]{:S(2)}) collective-permute-start(bf16[512,384]{1,0:T(8,128)(2,1)S(1)} %collective-permute-done.6.refs_0_), channel_id=1, source_target_pairs={{0,96},{32,0},{64,32},{96,64},{1,97},{33,1},{65,33},{97,65},{2,98}... | collective-permute-start | bytes 1179656 | tf_op jit(solution)/shard_map/ppermute | solution.py:19
  86.1 14.2 %collective-permute-start.10 = (bf16[1536,128]{1,0:T(8,128)(2,1)S(1)}, bf16[1536,128]{1,0:T(8,128)(2,1)S(1)}, u32[]{:S(2)}, u32[]{:S(2)}) collective-permute-start(bf16[1536,128]{1,0:T(8,128)(2,1)S(1)} %get-tuple-element.23), channel_id=1, source_target_pairs={{0,2},{2,0},{1,3},{3,1},{4,6},{6,4},{5,7},{7,5},{8,10},{10,8},{9,1... | collective-permute-start | bytes 1179656 | tf_op jit(solution)/shard_map/ppermute | solution.py:26
  87.2 13.3 %collective-permute-start.3 = (bf16[1536,128]{1,0:T(8,128)(2,1)S(1)}, bf16[1536,128]{1,0:T(8,128)(2,1)S(1)}, u32[]{:S(2)}, u32[]{:S(2)}) collective-permute-start(bf16[1536,128]{1,0:T(8,128)(2,1)S(1)} %get-tuple-element.22.refs_0_), channel_id=1, source_target_pairs={{0,8},{8,16},{16,24},{24,0},{1,9},{9,17},{17,25},{25,1},{2,10},{10... | collective-permute-start | bytes 1179656 | tf_op jit(solution)/shard_map/ppermute | solution.py:19
  89.7 13.4 %collective-permute-start.4 = (bf16[1536,128]{1,0:T(8,128)(2,1)S(1)}, bf16[1536,128]{1,0:T(8,128)(2,1)S(1)}, u32[]{:S(2)}, u32[]{:S(2)}) collective-permute-start(bf16[1536,128]{1,0:T(8,128)(2,1)S(1)} %get-tuple-element.22.refs_0_), channel_id=1, source_target_pairs={{0,24},{8,0},{16,8},{24,16},{1,25},{9,1},{17,9},{25,17},{2,26},{10... | collective-permute-start | bytes 1179656 | tf_op jit(solution)/shard_map/ppermute | solution.py:19
  94.2 33.9 %collective-permute-start.36 = (f32[2,512,256]{2,1,0:T(8,128)S(1)}, f32[2,512,256]{2,1,0:T(8,128)S(1)}, u32[]{:S(2)}, u32[]{:S(2)}) collective-permute-start(f32[2,512,256]{2,1,0:T(8,128)S(1)} %shard_map.64), channel_id=1, source_target_pairs={{0,1},{1,0},{2,3},{3,2},{4,5},{5,4},{6,7},{7,6},{8,9},{9,8},{10,11... | collective-permute-start | bytes 3145736 | tf_op jit(solution)/shard_map/ppermute | solution.py:244
  100.2 33.4 %collective-permute-start.34 = (f32[2,512,256]{2,1,0:T(8,128)S(1)}, f32[2,512,256]{2,1,0:T(8,128)S(1)}, u32[]{:S(2)}, u32[]{:S(2)}) collective-permute-start(f32[2,512,256]{2,1,0:T(8,128)S(1)} %shard_map.60), channel_id=1, source_target_pairs={{0,1},{1,0},{2,3},{3,2},{4,5},{5,4},{6,7},{7,6},{8,9},{9,8},{10,11... | collective-permute-start | bytes 3145736 | tf_op jit(solution)/shard_map/ppermute | solution.py:244
  103.1 13.1 %collective-permute-start.5 = (bf16[1536,128]{1,0:T(8,128)(2,1)S(1)}, bf16[1536,128]{1,0:T(8,128)(2,1)S(1)}, u32[]{:S(2)}, u32[]{:S(2)}) collective-permute-start(bf16[1536,128]{1,0:T(8,128)(2,1)S(1)} %shard_map.40), channel_id=1, source_target_pairs={{0,8},{1,25},{8,16},{9,1},{16,24},{17,9},{24,0},{25,17},{2,10},{3,... | collective-permute-start | bytes 1179656 | tf_op jit(solution)/shard_map/ppermute | solution.py:71
  120.2 15.9 %collective-permute-start.15 = (f32[2,512,128]{2,1,0:T(8,128)S(1)}, f32[2,512,128]{2,1,0:T(8,128)S(1)}, u32[]{:S(2)}, u32[]{:S(2)}) collective-permute-start(f32[2,512,128]{2,1,0:T(8,128)S(1)} %shard_map.46), channel_id=1, source_target_pairs={{0,1},{1,0},{2,3},{3,2},{4,5},{5,4},{6,7},{7,6},{8,9},{9,8},{10,11... | collective-permute-start | bytes 1572872 | tf_op jit(solution)/shard_map/ppermute | solution.py:244
  123.8 15.0 %collective-permute-start.23 = (f32[2,512,128]{2,1,0:T(8,128)S(1)}, f32[2,512,128]{2,1,0:T(8,128)S(1)}, u32[]{:S(2)}, u32[]{:S(2)}) collective-permute-start(f32[2,512,128]{2,1,0:T(8,128)S(1)} %shard_map.53), channel_id=1, source_target_pairs={{0,1},{1,0},{2,3},{3,2},{4,5},{5,4},{6,7},{7,6},{8,9},{9,8},{10,11... | collective-permute-start | bytes 1572872 | tf_op jit(solution)/shard_map/ppermute | solution.py:244
  131.2 15.3 %collective-permute-start.38 = (bf16[512,256]{1,0:T(8,128)(2,1)S(1)}, bf16[512,256]{1,0:T(8,128)(2,1)S(1)}, u32[]{:S(2)}, u32[]{:S(2)}) collective-permute-start(bf16[512,256]{1,0:T(8,128)(2,1)S(1)} %get-tuple-element.38), channel_id=1, source_target_pairs={{0,6},{2,4},{4,2},{6,0},{1,7},{3,5},{5,3},{7,1},{8,14},{10,12},{12... | collective-permute-start | bytes 786440 | tf_op jit(solution)/shard_map/ppermute | solution.py:27
  134.3 12.2 %collective-permute-start.35 = (bf16[512,256]{1,0:T(8,128)(2,1)S(1)}, bf16[512,256]{1,0:T(8,128)(2,1)S(1)}, u32[]{:S(2)}, u32[]{:S(2)}) collective-permute-start(bf16[512,256]{1,0:T(8,128)(2,1)S(1)} %get-tuple-element.36), channel_id=1, source_target_pairs={{0,2},{2,0},{1,3},{3,1},{4,6},{6,4},{5,7},{7,5},{8,10},{10,8},{9,1... | collective-permute-start | bytes 786440 | tf_op jit(solution)/shard_map/ppermute | solution.py:26
  (17 other events, 179.9 us)
